TPU v7x, 32 devices: a whole 2x2x4 slice. The times are simulated.
32 devices in a mesh: groups: 2 (over x), expert: 16 (over z, y, core).
Axes of the slice: x: 2, y: 2, z: 4, core: 2. Of those that a mesh axis runs over, the one named last changes fastest.
Arguments:
- tokens: bfloat16 [256, 6144], P(('groups', 'expert')), parts along dimension 0, may hold values from -6 to 6
- norm_gain: float32 [6144], replicated, may hold values from 0.5 to 1.5
- router: bfloat16 [6144, 4], replicated, may hold values from -0.078125 to 0.078125
- w_gate: bfloat16 [6144, 4096], P(None, 'expert'), may hold values from -0.078125 to 0.078125
- w_up: bfloat16 [6144, 4096], P(None, 'expert'), may hold values from -0.078125 to 0.078125
- w_down: bfloat16 [4096, 6144], P('expert'), may hold values from -0.1875 to 0.1875
- expert_ids: int32 [256, 2], P(('groups', 'expert')), parts along dimension 0, may hold values from 0 to 3, as said below
- live_rows: int32 [32], P(('groups', 'expert')), parts along dimension 0, may hold values from 6 to 8, as said below
Outputs:
- mixed_out: bfloat16 [256, 6144], P(('groups', 'expert')), parts along dimension 0
There are 2 independent parts, one for each index of `groups`. A program takes and returns all parts, laid end to end along the dimension named above; an argument that names none is the same for every part. Nothing has to cross between parts.
Inputs may be any that keep to these rules, and one draw needn't show every extreme that they name: `expert_ids`: each row names two different experts. Among the live rows of one device no expert is named by more than 6 rows; in every draw some expert is named by exactly 6 live rows of every device. `live_rows`: rows at or beyond this count in a device's block are padding; some device is full in every draw.
All inputs are finite; a program needn't handle non-finite values.
Results may differ from a plain program's by a relative error of at most 0.0042.
Values may be sent and summed in bfloat16 or wider, within the bound.
No kernel may reach another device: no remote copies, remote signals or barrier semaphores. Data moves between devices by JAX's collectives and lax.ppermute only.
A program may use at most 128 MiB of HBM per device.

v0:
```python
import functools

import jax
import jax.numpy as jnp
from jax import lax
from jax.experimental import pallas as pl
from jax.experimental.pallas import tpu as pltpu
from jax.sharding import PartitionSpec as P


CAP = 6
SUB = 8
EPS = 1e-05
CORES = 2
F32 = jnp.float32
BF16 = jnp.bfloat16


VMEM = pl.BlockSpec(memory_space=pltpu.VMEM)
SMEM = pl.BlockSpec(memory_space=pltpu.SMEM)


def near(value):
    return pltpu.with_memory_space_constraint(value, pltpu.VMEM)


def room(mebibytes):
    return pltpu.CompilerParams(vmem_limit_bytes=mebibytes << 20)


def far(value):
    return pltpu.with_memory_space_constraint(value, pltpu.HBM)


def dot(a, b):
    return jnp.dot(a, b, preferred_element_type=F32)


def packing(width):
    main = width * CAP // SUB
    tail = width - main
    blocks = main // tail
    return main, tail, blocks


def pre_kernel(experts, z_ref, live_ref, ids_ref, tok_ref, gain_ref, router_ref, *outs):
    pieces, table_ref = outs[:-1], outs[-1]
    rows, width = tok_ref.shape
    main, tail, blocks = packing(width)
    lanes = table_ref.shape[1]
    tok = tok_ref[...].astype(F32)
    scale = lax.rsqrt(jnp.mean(tok * tok, axis=-1, keepdims=True) + EPS)
    normed = (tok * scale * gain_ref[...]).astype(BF16)
    normed_f32 = normed.astype(F32)

    row = lax.broadcasted_iota(jnp.int32, (rows, lanes), 0)
    lane = lax.broadcasted_iota(jnp.int32, (rows, lanes), 1)
    first = jnp.zeros((rows, lanes), jnp.int32)
    second = jnp.zeros((rows, lanes), jnp.int32)
    for t in range(rows):
        first = jnp.where(row == t, ids_ref[0, t], first)
        second = jnp.where(row == t, ids_ref[1, t], second)
    alive = row < live_ref[0]
    logits = [
        jnp.sum(normed_f32 * router_ref[e : e + 1, :].astype(F32), axis=-1, keepdims=True)
        for e in range(experts)
    ]
    logit_first = jnp.zeros((rows, lanes), F32)
    logit_second = jnp.zeros((rows, lanes), F32)
    for e in range(experts):
        logit_first = jnp.where(first == e, logits[e], logit_first)
        logit_second = jnp.where(second == e, logits[e], logit_second)
    prob_first = 1.0 / (1.0 + jnp.exp(logit_second - logit_first))
    prob_second = 1.0 / (1.0 + jnp.exp(logit_first - logit_second))

    r = lane % SUB
    k = (lane // SUB) % experts
    j = lane // (SUB * experts)
    expert = k ^ z_ref[0]
    is_first = first == expert
    is_second = second == expert
    member = jnp.logical_and(jnp.logical_or(is_first, is_second), alive).astype(F32)
    slot = jnp.zeros((rows, lanes), F32)
    for t in range(rows - 1):
        slot = slot + jnp.where(row > t, member[t : t + 1, :], 0.0)
    main_slot = jnp.where(r < CAP, r, SUB)
    tail_slot = jnp.where(r < CAP, SUB, (r - CAP) * blocks + j - 1)
    wanted = jnp.where(j == 0, main_slot, tail_slot).astype(F32)
    placed = jnp.where(slot == wanted, member, 0.0)
    gate = jnp.where(is_first, prob_first, prob_second)
    table_ref[...] = placed * gate

    step = experts * SUB
    pick = placed.astype(BF16)
    for i in range(blocks):
        both = jnp.concatenate([pick[:, :step], pick[:, (1 + i) * step : (2 + i) * step]], axis=0)
        data = jnp.concatenate([normed[:, i * tail : (i + 1) * tail], normed[:, main:]], axis=0)
        block = lax.dot_general(both, data, (((0,), (0,)), ((), ())), preferred_element_type=F32).astype(BF16)
        for n, piece in enumerate(pieces):
            piece[:, i * tail : (i + 1) * tail] = block[n * SUB : (n + 1) * SUB, :]


def pre(tokens, norm_gain, router, expert_ids, live_rows, plane):
    rows, width = tokens.shape
    experts = router.shape[1]
    main, _, blocks = packing(width)
    lanes = (1 + blocks) * experts * SUB
    return pl.pallas_call(
        functools.partial(pre_kernel, experts),
        out_shape=[pltpu.VMEM((SUB, main), BF16)] * experts + [pltpu.VMEM((rows, lanes), F32)],
        in_specs=[SMEM, SMEM, SMEM, VMEM, VMEM, VMEM],
        out_specs=[VMEM] * (experts + 1),
        compiler_params=room(8),
        cost_estimate=pl.CostEstimate(flops=20 * 10**9, bytes_accessed=40 * 10**6, transcendentals=0),
        name="pre",
    )(plane.reshape(1), live_rows, far(expert_ids.T), far(tokens), far(norm_gain.reshape(1, width)), far(router.T))


def ffn_kernel(count, *refs):
    pieces = refs[:count]
    wg_ref, wu_ref, wd_ref = refs[count : count + 3]
    outs, x_ref = refs[count + 3 : -1], refs[-1]
    width = wg_ref.shape[0]
    hidden_width = wg_ref.shape[1]
    main, tail, blocks = packing(width)
    at = 0
    for piece in pieces:
        n = piece.shape[0]
        x_ref[at : at + n, :] = piece[...]
        at += n
    total = at
    size = 128 if total % 128 == 0 else total
    row = lax.broadcasted_iota(jnp.int32, (size, size), 0)
    col = lax.broadcasted_iota(jnp.int32, (size, size), 1)
    same = row // SUB == col // SUB
    in_row = lax.broadcasted_iota(jnp.int32, (size, hidden_width), 0) % SUB

    def chunk(base):
        x = x_ref[pl.ds(base, size), :]
        rest = jnp.zeros((size, tail), F32)
        for i in range(blocks):
            take = jnp.logical_and(same, row % SUB == (col % SUB - CAP) * blocks + i)
            take = jnp.logical_and(take, col % SUB >= CAP)
            rest = rest + dot(take.astype(BF16), x[:, i * tail : (i + 1) * tail])
        rest = rest.astype(BF16)
        gate = dot(x, wg_ref[:main, :]) + dot(rest, wg_ref[main:, :])
        up = dot(x, wu_ref[:main, :]) + dot(rest, wu_ref[main:, :])
        hidden = (gate / (1.0 + jnp.exp(-gate)) * up).astype(BF16)
        upper = jnp.where(in_row < CAP, hidden, jnp.zeros_like(hidden))
        for i in range(blocks):
            give = jnp.logical_and(same, col % SUB == (row % SUB - CAP) * blocks + i)
            give = jnp.logical_and(give, row % SUB >= CAP)
            lower = dot(give.astype(BF16), hidden).astype(BF16)
            cols = slice(i * tail, (i + 1) * tail)
            out = (dot(upper, wd_ref[:, cols]) + dot(lower, wd_ref[:, main:])).astype(BF16)
            x_ref[pl.ds(base, size), cols] = out

    if total == size:
        chunk(0)
    else:
        lax.fori_loop(0, total // size, lambda n, c: (chunk(pl.multiple_of(n * size, size)), c)[1], 0)
    at = 0
    for out in outs:
        n = out.shape[0]
        out[...] = x_ref[at : at + n, :]
        at += n


def ffn(pieces, weights, sizes):
    total, main = sum(sizes), pieces[0].shape[1]
    return pl.pallas_call(
        functools.partial(ffn_kernel, len(pieces)),
        out_shape=[pltpu.VMEM((n, main), BF16) for n in sizes],
        in_specs=[VMEM] * (len(pieces) + 3),
        out_specs=[VMEM] * len(sizes),
        scratch_shapes=[pltpu.VMEM((total, main), BF16)],
        compiler_params=room(16),
        name="ffn",
    )(*map(near, pieces), *map(near, weights))


def add_kernel(count, *refs):
    total = refs[0][...].astype(F32)
    for ref in refs[1:count]:
        total = total + ref[...].astype(F32)
    at = 0
    for out in refs[count:]:
        n = out.shape[0]
        out[...] = total[at : at + n, :].astype(BF16)
        at += n


def add(terms, parts):
    rows, main = terms[0].shape
    return pl.pallas_call(
        functools.partial(add_kernel, len(terms)),
        out_shape=[pltpu.VMEM((rows // parts, main), BF16)] * parts,
        in_specs=[VMEM] * len(terms),
        out_specs=[VMEM] * parts,
        compiler_params=room(4),
        name="add",
    )(*map(near, terms))


def combine_kernel(experts, table_ref, tok_ref, *refs):
    pieces, out_ref = refs[:-1], refs[-1]
    own, others = pieces[: 1 - experts], [p[...] for p in pieces[1 - experts :]]
    width = tok_ref.shape[1]
    main, tail, blocks = packing(width)
    step = experts * SUB
    table = table_ref[...]
    high = table.astype(BF16)
    low = (table - high.astype(F32)).astype(BF16)
    first = own[0][...].astype(F32)
    for ref in own[1:]:
        first = first + ref[...].astype(F32)
    arrived = [first.astype(BF16)] + others
    rest = jnp.zeros((tok_ref.shape[0], tail), F32)
    for i in range(blocks):
        cols = slice(i * tail, (i + 1) * tail)
        data = jnp.concatenate([p[:, cols] for p in arrived], axis=0)
        mine, theirs = slice(0, step), slice((1 + i) * step, (2 + i) * step)
        out_ref[:, cols] = (
            tok_ref[:, cols].astype(F32) + dot(high[:, mine], data) + dot(low[:, mine], data)
        ).astype(BF16)
        rest = rest + dot(high[:, theirs], data) + dot(low[:, theirs], data)
    out_ref[:, main:] = (tok_ref[:, main:].astype(F32) + rest).astype(BF16)


def combine(experts, table, tokens, pieces):
    return pl.pallas_call(
        functools.partial(combine_kernel, experts),
        out_shape=jax.ShapeDtypeStruct(tokens.shape, BF16),
        in_specs=[VMEM] * (2 + len(pieces)),
        out_specs=VMEM,
        compiler_params=room(8),
        name="combine",
    )(near(table), near(tokens), *map(near, pieces))


def local(tokens, norm_gain, router, w_gate, w_up, w_down, expert_ids, live_rows):
    devices = lax.axis_size("expert")
    experts = router.shape[1]
    members = devices // experts
    lines = members // CORES

    def swap(value, distance):
        return lax.ppermute(value, "expert", [(i, i ^ distance) for i in range(devices)])

    plane = lax.axis_index("expert") // members
    *outgoing, table = pre(tokens, norm_gain, router, expert_ids, live_rows, plane)
    weights = [w_gate, w_up, w_down]

    here = {}
    for k in range(experts):
        here[0, k, 0] = swap(outgoing[k], k * members) if k else outgoing[0]
    for k in range(experts):
        for y in range(1, lines):
            here[0, k, y] = swap(here[0, k, 0], y * CORES)
    for k in range(experts):
        for y in range(lines):
            here[1, k, y] = swap(here[0, k, y], 1)
    groups = [list(range(experts // 2, experts)), list(range(experts // 2 - 1, -1, -1))]
    order = [(c, k, y) for c in range(CORES) for g in groups for k in g for y in range(lines)]
    results = ffn([here[o] for o in order], weights, [len(g) * lines * SUB for _ in range(CORES) for g in groups])

    half = {}
    for n, group in enumerate(groups):
        keep, give = results[n], results[len(groups) + n]
        parts = add([keep, swap(give, 1)], len(group) * lines)
        for m, k in enumerate(group):
            mine, theirs = parts[m * lines], parts[m * lines + 1 : (m + 1) * lines]
            half[k] = [mine] + [swap(p, (y + 1) * CORES) for y, p in enumerate(theirs)]
    home = list(half[0])
    for k in range(1, experts):
        (total,) = add(half[k], 1)
        home.append(swap(total, k * members))
    return combine(experts, table, tokens, home)


def solution(mesh):
    return jax.shard_map(
        local,
        mesh=mesh,
        in_specs=(
            P(("groups", "expert"), None),
            P(),
            P(),
            P(None, "expert"),
            P(None, "expert"),
            P("expert", None),
            P(("groups", "expert"), None),
            P(("groups", "expert")),
        ),
        out_specs=P(("groups", "expert"), None),
        check_vma=False,
    )
```

profile of v0, /device:TPU:0, one launch (start us, length us, event | category | flops | bytes accessed | tf_op | source)
XLA Modules:
  0.0 43.2 jit_solution(6032387860821411118)
XLA Ops:
  0.7 0.0 copy-start
  0.7 0.0 copy-start.1
  0.7 0.0 copy-start.2
  0.7 1.5 %pre.1 = (bf16[8,4608]{1,0:T(8,128)(2,1)S(1)}, bf16[8,4608]{1,0:T(8,128)(2,1)S(1)}, bf16[8,4608]{1,0:T(8,128)(2,1)S(1)}, bf16[8,4608]{1,0:T(8,128)(2,1)S(1)}, f32[8,128]{1,0:T(8,128)S(1)}) custom-call(s32[1]{0:T(128)} %bitcast.z_ref, s32[1]{0:T(128)S(6)} %copy.9.live_ref, s32[2,8]{1,0:T(2,128)} %bitcast.6, bf16[8,6144]{1,0:T(8,128)(2,1)} %tok_ref.3, ...), custom_call_target="tpu_custom_call" | custom-call | flops 20000000000 | bytes 40000000 | tf_op jit(solution)/shard_map/pre/pallas_call | solution.py:108
  2.2 4.1 %collective-permute-start = (bf16[8,4608]{1,0:T(8,128)(2,1)S(1)}, bf16[8,4608]{1,0:T(8,128)(2,1)S(1)}, u32[]{:S(2)}, u32[]{:S(2)}) collective-permute-start(bf16[8,4608]{1,0:T(8,128)(2,1)S(1)} %get-tuple-element.23), channel_id=1, source_target_pairs={{0,8},{1,9},{2,10},{3,11},{4,12},{5,13},{6,14},{7,15},{8,0},{9,1},... | collective-permute-start | bytes 221192 | tf_op jit(solution)/shard_map/ppermute | solution.py:248
  6.3 1.3 %collective-permute-start.2 = (bf16[8,4608]{1,0:T(8,128)(2,1)S(1)}, bf16[8,4608]{1,0:T(8,128)(2,1)S(1)}, u32[]{:S(2)}, u32[]{:S(2)}) collective-permute-start(bf16[8,4608]{1,0:T(8,128)(2,1)S(1)} %get-tuple-element.24), channel_id=1, source_target_pairs={{0,12},{1,13},{2,14},{3,15},{4,8},{5,9},{6,10},{7,11},{8,4},{9,5},... | collective-permute-start | bytes 221192 | tf_op jit(solution)/shard_map/ppermute | solution.py:248
  7.6 0.2 collective-permute-start.4
  7.9 0.0 copy-start.3
  7.9 0.0 collective-permute-start.13
  7.9 1.5 %collective-permute-start.6 = (bf16[8,4608]{1,0:T(8,128)(2,1)S(1)}, bf16[8,4608]{1,0:T(8,128)(2,1)S(1)}, u32[]{:S(2)}, u32[]{:S(2)}) collective-permute-start(bf16[8,4608]{1,0:T(8,128)(2,1)S(1)} %get-tuple-element.26.refs_6_), channel_id=1, source_target_pairs={{0,2},{1,3},{2,0},{3,1},{4,6},{5,7},{6,4},{7,5},{8,10},{9,11},{10,... | collective-permute-start | bytes 221192 | tf_op jit(solution)/shard_map/ppermute | solution.py:248
  9.4 1.8 %collective-permute-done.refs_0_ = bf16[8,4608]{1,0:T(8,128)(2,1)S(1)} collective-permute-done((bf16[8,4608]{1,0:T(8,128)(2,1)S(1)}, bf16[8,4608]{1,0:T(8,128)(2,1)S(1)}, u32[]{:S(2)}, u32[]{:S(2)}) %collective-permute-start) | collective-permute-done | bytes 73760 | tf_op jit(solution)/shard_map/ppermute | solution.py:248
  11.2 0.0 collective-permute-start.7
  11.2 1.5 %collective-permute-done.2.refs_2_ = bf16[8,4608]{1,0:T(8,128)(2,1)S(1)} collective-permute-done((bf16[8,4608]{1,0:T(8,128)(2,1)S(1)}, bf16[8,4608]{1,0:T(8,128)(2,1)S(1)}, u32[]{:S(2)}, u32[]{:S(2)}) %collective-permute-start.2) | collective-permute-done | bytes 73760 | tf_op jit(solution)/shard_map/ppermute | solution.py:248
  12.7 1.5 %collective-permute-start.1 = (bf16[8,4608]{1,0:T(8,128)(2,1)S(1)}, bf16[8,4608]{1,0:T(8,128)(2,1)S(1)}, u32[]{:S(2)}, u32[]{:S(2)}) collective-permute-start(bf16[8,4608]{1,0:T(8,128)(2,1)S(1)} %collective-permute-done.refs_0_), channel_id=1, source_target_pairs={{0,2},{1,3},{2,0},{3,1},{4,6},{5,7},{6,4},{7,5},{8,10},{9,11},{10,... | collective-permute-start | bytes 221192 | tf_op jit(solution)/shard_map/ppermute | solution.py:248
  14.2 0.0 collective-permute-done.4.refs_4_
  14.2 0.0 collective-permute-start.9
  14.2 0.0 collective-permute-done.13.refs_14_
  14.2 0.6 %collective-permute-start.3 = (bf16[8,4608]{1,0:T(8,128)(2,1)S(1)}, bf16[8,4608]{1,0:T(8,128)(2,1)S(1)}, u32[]{:S(2)}, u32[]{:S(2)}) collective-permute-start(bf16[8,4608]{1,0:T(8,128)(2,1)S(1)} %collective-permute-done.2.refs_2_), channel_id=1, source_target_pairs={{0,2},{1,3},{2,0},{3,1},{4,6},{5,7},{6,4},{7,5},{8,10},{9,11},{10,... | collective-permute-start | bytes 221192 | tf_op jit(solution)/shard_map/ppermute | solution.py:248
  14.8 0.0 collective-permute-done.6.refs_7_
  14.8 1.5 %collective-permute-start.5 = (bf16[8,4608]{1,0:T(8,128)(2,1)S(1)}, bf16[8,4608]{1,0:T(8,128)(2,1)S(1)}, u32[]{:S(2)}, u32[]{:S(2)}) collective-permute-start(bf16[8,4608]{1,0:T(8,128)(2,1)S(1)} %collective-permute-done.4.refs_4_), channel_id=1, source_target_pairs={{0,2},{1,3},{2,0},{3,1},{4,6},{5,7},{6,4},{7,5},{8,10},{9,11},{10,... | collective-permute-start | bytes 221192 | tf_op jit(solution)/shard_map/ppermute | solution.py:248
  16.3 0.0 collective-permute-done.7.refs_8_
  16.3 0.0 collective-permute-start.11
  16.3 0.7 %collective-permute-done.1.refs_1_ = bf16[8,4608]{1,0:T(8,128)(2,1)S(1)} collective-permute-done((bf16[8,4608]{1,0:T(8,128)(2,1)S(1)}, bf16[8,4608]{1,0:T(8,128)(2,1)S(1)}, u32[]{:S(2)}, u32[]{:S(2)}) %collective-permute-start.1) | collective-permute-done | bytes 73760 | tf_op jit(solution)/shard_map/ppermute | solution.py:248
  17.1 0.0 collective-permute-start.14
  17.1 0.0 collective-permute-done.9.refs_10_
  17.1 0.5 %collective-permute-start.8 = (bf16[8,4608]{1,0:T(8,128)(2,1)S(1)}, bf16[8,4608]{1,0:T(8,128)(2,1)S(1)}, u32[]{:S(2)}, u32[]{:S(2)}) collective-permute-start(bf16[8,4608]{1,0:T(8,128)(2,1)S(1)} %collective-permute-done.1.refs_1_), channel_id=1, source_target_pairs={{0,1},{1,0},{2,3},{3,2},{4,5},{5,4},{6,7},{7,6},{8,9},{9,8},{10,11... | collective-permute-start | bytes 221192 | tf_op jit(solution)/shard_map/ppermute | solution.py:248
  17.6 1.9 %collective-permute-done.3.refs_3_ = bf16[8,4608]{1,0:T(8,128)(2,1)S(1)} collective-permute-done((bf16[8,4608]{1,0:T(8,128)(2,1)S(1)}, bf16[8,4608]{1,0:T(8,128)(2,1)S(1)}, u32[]{:S(2)}, u32[]{:S(2)}) %collective-permute-start.3) | collective-permute-done | bytes 73760 | tf_op jit(solution)/shard_map/ppermute | solution.py:248
  19.4 0.0 collective-permute-start.10
  19.5 1.0 %collective-permute-done.5.refs_5_ = bf16[8,4608]{1,0:T(8,128)(2,1)S(1)} collective-permute-done((bf16[8,4608]{1,0:T(8,128)(2,1)S(1)}, bf16[8,4608]{1,0:T(8,128)(2,1)S(1)}, u32[]{:S(2)}, u32[]{:S(2)}) %collective-permute-start.5) | collective-permute-done | bytes 73760 | tf_op jit(solution)/shard_map/ppermute | solution.py:248
  20.5 0.0 collective-permute-start.12
  20.5 0.0 collective-permute-done.11.refs_12_
  20.5 0.0 collective-permute-done.14.refs_15_
  20.5 0.0 collective-permute-done.8.refs_9_
  20.5 0.2 collective-permute-done.10.refs_11_
  20.7 1.1 %collective-permute-done.12.refs_13_ = bf16[8,4608]{1,0:T(8,128)(2,1)S(1)} collective-permute-done((bf16[8,4608]{1,0:T(8,128)(2,1)S(1)}, bf16[8,4608]{1,0:T(8,128)(2,1)S(1)}, u32[]{:S(2)}, u32[]{:S(2)}) %collective-permute-start.12) | collective-permute-done | bytes 73760 | tf_op jit(solution)/shard_map/ppermute | solution.py:248
  21.8 0.0 copy-done
  21.8 0.0 copy-done.1
  21.8 0.0 copy-done.2
  21.8 2.5 %ffn.1 = (bf16[32,4608]{1,0:T(8,128)(2,1)S(1)}, bf16[32,4608]{1,0:T(8,128)(2,1)S(1)}, bf16[32,4608]{1,0:T(8,128)(2,1)S(1)}, bf16[32,4608]{1,0:T(8,128)(2,1)S(1)}) custom-call(bf16[8,4608]{1,0:T(8,128)(2,1)S(1)} %collective-permute-done.refs_0_, bf16[8,4608]{1,0:T(8,128)(2,1)S(1)} %collective-permute-done.1.refs_1_, ...), custom_call_target="tpu_custom_call" | custom-call | tf_op jit(solution)/shard_map/ffn/pallas_call | solution.py:171
  24.3 0.2 collective-permute-start.15
  24.5 0.4 collective-permute-start.19
  24.8 1.1 %collective-permute-done.15.refs_1_ = bf16[32,4608]{1,0:T(8,128)(2,1)S(1)} collective-permute-done((bf16[32,4608]{1,0:T(8,128)(2,1)S(1)}, bf16[32,4608]{1,0:T(8,128)(2,1)S(1)}, u32[]{:S(2)}, u32[]{:S(2)}) %collective-permute-start.15) | collective-permute-done | bytes 294944 | tf_op jit(solution)/shard_map/ppermute | solution.py:248
  25.9 0.1 add.6
  26.0 1.3 %collective-permute-start.17 = (bf16[8,4608]{1,0:T(8,128)(2,1)S(1)}, bf16[8,4608]{1,0:T(8,128)(2,1)S(1)}, u32[]{:S(2)}, u32[]{:S(2)}) collective-permute-start(bf16[8,4608]{1,0:T(8,128)(2,1)S(1)} %get-tuple-element.32), channel_id=1, source_target_pairs={{0,2},{1,3},{2,0},{3,1},{4,6},{5,7},{6,4},{7,5},{8,10},{9,11},{10,... | collective-permute-start | bytes 221192 | tf_op jit(solution)/shard_map/ppermute | solution.py:248
  27.3 0.0 collective-permute-done.19.refs_1_
  27.3 0.1 add.8
  27.4 0.9 %collective-permute-start.20 = (bf16[8,4608]{1,0:T(8,128)(2,1)S(1)}, bf16[8,4608]{1,0:T(8,128)(2,1)S(1)}, u32[]{:S(2)}, u32[]{:S(2)}) collective-permute-start(bf16[8,4608]{1,0:T(8,128)(2,1)S(1)} %get-tuple-element.36), channel_id=1, source_target_pairs={{0,2},{1,3},{2,0},{3,1},{4,6},{5,7},{6,4},{7,5},{8,10},{9,11},{10,... | collective-permute-start | bytes 221192 | tf_op jit(solution)/shard_map/ppermute | solution.py:248
  28.2 1.2 %collective-permute-start.22 = (bf16[8,4608]{1,0:T(8,128)(2,1)S(1)}, bf16[8,4608]{1,0:T(8,128)(2,1)S(1)}, u32[]{:S(2)}, u32[]{:S(2)}) collective-permute-start(bf16[8,4608]{1,0:T(8,128)(2,1)S(1)} %get-tuple-element.38), channel_id=1, source_target_pairs={{0,2},{1,3},{2,0},{3,1},{4,6},{5,7},{6,4},{7,5},{8,10},{9,11},{10,... | collective-permute-start | bytes 221192 | tf_op jit(solution)/shard_map/ppermute | solution.py:248
  29.5 0.8 %collective-permute-start.16 = (bf16[8,4608]{1,0:T(8,128)(2,1)S(1)}, bf16[8,4608]{1,0:T(8,128)(2,1)S(1)}, u32[]{:S(2)}, u32[]{:S(2)}) collective-permute-start(bf16[8,4608]{1,0:T(8,128)(2,1)S(1)} %get-tuple-element.30), channel_id=1, source_target_pairs={{0,2},{1,3},{2,0},{3,1},{4,6},{5,7},{6,4},{7,5},{8,10},{9,11},{10,... | collective-permute-start | bytes 221192 | tf_op jit(solution)/shard_map/ppermute | solution.py:248
  30.2 0.7 %collective-permute-done.17.refs_1_ = bf16[8,4608]{1,0:T(8,128)(2,1)S(1)} collective-permute-done((bf16[8,4608]{1,0:T(8,128)(2,1)S(1)}, bf16[8,4608]{1,0:T(8,128)(2,1)S(1)}, u32[]{:S(2)}, u32[]{:S(2)}) %collective-permute-start.17) | collective-permute-done | bytes 73760 | tf_op jit(solution)/shard_map/ppermute | solution.py:248
  30.9 1.5 %collective-permute-start.18 = (bf16[8,4608]{1,0:T(8,128)(2,1)S(1)}, bf16[8,4608]{1,0:T(8,128)(2,1)S(1)}, u32[]{:S(2)}, u32[]{:S(2)}) collective-permute-start(bf16[8,4608]{1,0:T(8,128)(2,1)S(1)} %add.7), channel_id=1, source_target_pairs={{0,4},{1,5},{2,6},{3,7},{4,0},{5,1},{6,2},{7,3},{8,12},{9,13},{10,... | collective-permute-start | bytes 221192 | tf_op jit(solution)/shard_map/ppermute | solution.py:248
  32.4 0.1 collective-permute-done.20.refs_1_
  32.6 3.3 %collective-permute-start.21 = (bf16[8,4608]{1,0:T(8,128)(2,1)S(1)}, bf16[8,4608]{1,0:T(8,128)(2,1)S(1)}, u32[]{:S(2)}, u32[]{:S(2)}) collective-permute-start(bf16[8,4608]{1,0:T(8,128)(2,1)S(1)} %add.9), channel_id=1, source_target_pairs={{0,8},{1,9},{2,10},{3,11},{4,12},{5,13},{6,14},{7,15},{8,0},{9,1},... | collective-permute-start | bytes 221192 | tf_op jit(solution)/shard_map/ppermute | solution.py:248
  35.9 0.0 collective-permute-done.22.refs_1_
  36.0 1.4 %collective-permute-start.23 = (bf16[8,4608]{1,0:T(8,128)(2,1)S(1)}, bf16[8,4608]{1,0:T(8,128)(2,1)S(1)}, u32[]{:S(2)}, u32[]{:S(2)}) collective-permute-start(bf16[8,4608]{1,0:T(8,128)(2,1)S(1)} %add.10), channel_id=1, source_target_pairs={{0,12},{1,13},{2,14},{3,15},{4,8},{5,9},{6,10},{7,11},{8,4},{9,5},... | collective-permute-start | bytes 221192 | tf_op jit(solution)/shard_map/ppermute | solution.py:248
  37.4 0.0 collective-permute-done.16.refs_1_
  37.4 0.0 collective-permute-done.18.refs_2_
  37.4 3.1 %collective-permute-done.21.refs_3_ = bf16[8,4608]{1,0:T(8,128)(2,1)S(1)} collective-permute-done((bf16[8,4608]{1,0:T(8,128)(2,1)S(1)}, bf16[8,4608]{1,0:T(8,128)(2,1)S(1)}, u32[]{:S(2)}, u32[]{:S(2)}) %collective-permute-start.21) | collective-permute-done | bytes 73760 | tf_op jit(solution)/shard_map/ppermute | solution.py:248
  40.5 1.7 %collective-permute-done.23.refs_4_ = bf16[8,4608]{1,0:T(8,128)(2,1)S(1)} collective-permute-done((bf16[8,4608]{1,0:T(8,128)(2,1)S(1)}, bf16[8,4608]{1,0:T(8,128)(2,1)S(1)}, u32[]{:S(2)}, u32[]{:S(2)}) %collective-permute-start.23) | collective-permute-done | bytes 73760 | tf_op jit(solution)/shard_map/ppermute | solution.py:248
  42.2 0.0 copy-done.3
  42.2 1.0 %combine.1 = bf16[8,6144]{1,0:T(8,128)(2,1)} custom-call(f32[8,128]{1,0:T(8,128)S(1)} %get-tuple-element.22.table_ref, bf16[8,6144]{1,0:T(8,128)(2,1)S(1)} %copy-done.3, bf16[8,4608]{1,0:T(8,128)(2,1)S(1)} %get-tuple-element.29.refs_0_, bf16[8,4608]{1,0:T(8,128)(2,1)S(1)} %collective-permute-done.16.refs_1_, ...), custom_call_target="tpu_custom_call" | custom-call | tf_op jit(solution)/shard_map/combine/pallas_call | solution.py:231
  (3 shorter events, 0.1 us)
Async XLA Ops:
  0.7 21.1 %copy-start = (bf16[6144,256]{1,0:T(8,128)(2,1)S(1)}, bf16[6144,256]{1,0:T(8,128)(2,1)}, u32[]{:S(2)}) copy-start(bf16[6144,256]{1,0:T(8,128)(2,1)} %refs_16_.1) | copy-start | bytes 9437188
  0.7 21.1 %copy-start.1 = (bf16[6144,256]{1,0:T(8,128)(2,1)S(1)}, bf16[6144,256]{1,0:T(8,128)(2,1)}, u32[]{:S(2)}) copy-start(bf16[6144,256]{1,0:T(8,128)(2,1)} %refs_17_.1) | copy-start | bytes 9437188
  0.7 21.1 %copy-start.2 = (bf16[256,6144]{1,0:T(8,128)(2,1)S(1)}, bf16[256,6144]{1,0:T(8,128)(2,1)}, u32[]{:S(2)}) copy-start(bf16[256,6144]{1,0:T(8,128)(2,1)} %refs_18_.1) | copy-start | bytes 9437188
  2.2 9.1 %collective-permute-start = (bf16[8,4608]{1,0:T(8,128)(2,1)S(1)}, bf16[8,4608]{1,0:T(8,128)(2,1)S(1)}, u32[]{:S(2)}, u32[]{:S(2)}) collective-permute-start(bf16[8,4608]{1,0:T(8,128)(2,1)S(1)} %get-tuple-element.23), channel_id=1, source_target_pairs={{0,8},{1,9},{2,10},{3,11},{4,12},{5,13},{6,14},{7,15},{8,0},{9,1},... | collective-permute-start | bytes 221192 | tf_op jit(solution)/shard_map/ppermute | solution.py:248
  6.3 6.4 %collective-permute-start.2 = (bf16[8,4608]{1,0:T(8,128)(2,1)S(1)}, bf16[8,4608]{1,0:T(8,128)(2,1)S(1)}, u32[]{:S(2)}, u32[]{:S(2)}) collective-permute-start(bf16[8,4608]{1,0:T(8,128)(2,1)S(1)} %get-tuple-element.24), channel_id=1, source_target_pairs={{0,12},{1,13},{2,14},{3,15},{4,8},{5,9},{6,10},{7,11},{8,4},{9,5},... | collective-permute-start | bytes 221192 | tf_op jit(solution)/shard_map/ppermute | solution.py:248
  7.6 6.6 %collective-permute-start.4 = (bf16[8,4608]{1,0:T(8,128)(2,1)S(1)}, bf16[8,4608]{1,0:T(8,128)(2,1)S(1)}, u32[]{:S(2)}, u32[]{:S(2)}) collective-permute-start(bf16[8,4608]{1,0:T(8,128)(2,1)S(1)} %get-tuple-element.25), channel_id=1, source_target_pairs={{0,4},{1,5},{2,6},{3,7},{4,0},{5,1},{6,2},{7,3},{8,12},{9,13},{10,... | collective-permute-start | bytes 221192 | tf_op jit(solution)/shard_map/ppermute | solution.py:248
  7.9 34.3 %copy-start.3 = (bf16[8,6144]{1,0:T(8,128)(2,1)S(1)}, bf16[8,6144]{1,0:T(8,128)(2,1)}, u32[]{:S(2)}) copy-start(bf16[8,6144]{1,0:T(8,128)(2,1)} %tok_ref.3) | copy-start | bytes 294916
  7.9 6.4 %collective-permute-start.13 = (bf16[8,4608]{1,0:T(8,128)(2,1)S(1)}, bf16[8,4608]{1,0:T(8,128)(2,1)S(1)}, u32[]{:S(2)}, u32[]{:S(2)}) collective-permute-start(bf16[8,4608]{1,0:T(8,128)(2,1)S(1)} %get-tuple-element.26.refs_6_), channel_id=1, source_target_pairs={{0,1},{1,0},{2,3},{3,2},{4,5},{5,4},{6,7},{7,6},{8,9},{9,8},{10,11... | collective-permute-start | bytes 221192 | tf_op jit(solution)/shard_map/ppermute | solution.py:248
  7.9 6.9 %collective-permute-start.6 = (bf16[8,4608]{1,0:T(8,128)(2,1)S(1)}, bf16[8,4608]{1,0:T(8,128)(2,1)S(1)}, u32[]{:S(2)}, u32[]{:S(2)}) collective-permute-start(bf16[8,4608]{1,0:T(8,128)(2,1)S(1)} %get-tuple-element.26.refs_6_), channel_id=1, source_target_pairs={{0,2},{1,3},{2,0},{3,1},{4,6},{5,7},{6,4},{7,5},{8,10},{9,11},{10,... | collective-permute-start | bytes 221192 | tf_op jit(solution)/shard_map/ppermute | solution.py:248
  11.2 5.1 %collective-permute-start.7 = (bf16[8,4608]{1,0:T(8,128)(2,1)S(1)}, bf16[8,4608]{1,0:T(8,128)(2,1)S(1)}, u32[]{:S(2)}, u32[]{:S(2)}) collective-permute-start(bf16[8,4608]{1,0:T(8,128)(2,1)S(1)} %collective-permute-done.refs_0_), channel_id=1, source_target_pairs={{0,1},{1,0},{2,3},{3,2},{4,5},{5,4},{6,7},{7,6},{8,9},{9,8},{10,11... | collective-permute-start | bytes 221192 | tf_op jit(solution)/shard_map/ppermute | solution.py:248
  12.7 4.4 %collective-permute-start.1 = (bf16[8,4608]{1,0:T(8,128)(2,1)S(1)}, bf16[8,4608]{1,0:T(8,128)(2,1)S(1)}, u32[]{:S(2)}, u32[]{:S(2)}) collective-permute-start(bf16[8,4608]{1,0:T(8,128)(2,1)S(1)} %collective-permute-done.refs_0_), channel_id=1, source_target_pairs={{0,2},{1,3},{2,0},{3,1},{4,6},{5,7},{6,4},{7,5},{8,10},{9,11},{10,... | collective-permute-start | bytes 221192 | tf_op jit(solution)/shard_map/ppermute | solution.py:248
  14.2 2.8 %collective-permute-start.9 = (bf16[8,4608]{1,0:T(8,128)(2,1)S(1)}, bf16[8,4608]{1,0:T(8,128)(2,1)S(1)}, u32[]{:S(2)}, u32[]{:S(2)}) collective-permute-start(bf16[8,4608]{1,0:T(8,128)(2,1)S(1)} %collective-permute-done.2.refs_2_), channel_id=1, source_target_pairs={{0,1},{1,0},{2,3},{3,2},{4,5},{5,4},{6,7},{7,6},{8,9},{9,8},{10,11... | collective-permute-start | bytes 221192 | tf_op jit(solution)/shard_map/ppermute | solution.py:248
  14.2 5.2 %collective-permute-start.3 = (bf16[8,4608]{1,0:T(8,128)(2,1)S(1)}, bf16[8,4608]{1,0:T(8,128)(2,1)S(1)}, u32[]{:S(2)}, u32[]{:S(2)}) collective-permute-start(bf16[8,4608]{1,0:T(8,128)(2,1)S(1)} %collective-permute-done.2.refs_2_), channel_id=1, source_target_pairs={{0,2},{1,3},{2,0},{3,1},{4,6},{5,7},{6,4},{7,5},{8,10},{9,11},{10,... | collective-permute-start | bytes 221192 | tf_op jit(solution)/shard_map/ppermute | solution.py:248
  14.8 5.7 %collective-permute-start.5 = (bf16[8,4608]{1,0:T(8,128)(2,1)S(1)}, bf16[8,4608]{1,0:T(8,128)(2,1)S(1)}, u32[]{:S(2)}, u32[]{:S(2)}) collective-permute-start(bf16[8,4608]{1,0:T(8,128)(2,1)S(1)} %collective-permute-done.4.refs_4_), channel_id=1, source_target_pairs={{0,2},{1,3},{2,0},{3,1},{4,6},{5,7},{6,4},{7,5},{8,10},{9,11},{10,... | collective-permute-start | bytes 221192 | tf_op jit(solution)/shard_map/ppermute | solution.py:248
  16.3 4.2 %collective-permute-start.11 = (bf16[8,4608]{1,0:T(8,128)(2,1)S(1)}, bf16[8,4608]{1,0:T(8,128)(2,1)S(1)}, u32[]{:S(2)}, u32[]{:S(2)}) collective-permute-start(bf16[8,4608]{1,0:T(8,128)(2,1)S(1)} %collective-permute-done.4.refs_4_), channel_id=1, source_target_pairs={{0,1},{1,0},{2,3},{3,2},{4,5},{5,4},{6,7},{7,6},{8,9},{9,8},{10,11... | collective-permute-start | bytes 221192 | tf_op jit(solution)/shard_map/ppermute | solution.py:248
  17.1 3.4 %collective-permute-start.14 = (bf16[8,4608]{1,0:T(8,128)(2,1)S(1)}, bf16[8,4608]{1,0:T(8,128)(2,1)S(1)}, u32[]{:S(2)}, u32[]{:S(2)}) collective-permute-start(bf16[8,4608]{1,0:T(8,128)(2,1)S(1)} %collective-permute-done.6.refs_7_), channel_id=1, source_target_pairs={{0,1},{1,0},{2,3},{3,2},{4,5},{5,4},{6,7},{7,6},{8,9},{9,8},{10,11... | collective-permute-start | bytes 221192 | tf_op jit(solution)/shard_map/ppermute | solution.py:248
  17.1 3.4 %collective-permute-start.8 = (bf16[8,4608]{1,0:T(8,128)(2,1)S(1)}, bf16[8,4608]{1,0:T(8,128)(2,1)S(1)}, u32[]{:S(2)}, u32[]{:S(2)}) collective-permute-start(bf16[8,4608]{1,0:T(8,128)(2,1)S(1)} %collective-permute-done.1.refs_1_), channel_id=1, source_target_pairs={{0,1},{1,0},{2,3},{3,2},{4,5},{5,4},{6,7},{7,6},{8,9},{9,8},{10,11... | collective-permute-start | bytes 221192 | tf_op jit(solution)/shard_map/ppermute | solution.py:248
  19.4 1.3 %collective-permute-start.10 = (bf16[8,4608]{1,0:T(8,128)(2,1)S(1)}, bf16[8,4608]{1,0:T(8,128)(2,1)S(1)}, u32[]{:S(2)}, u32[]{:S(2)}) collective-permute-start(bf16[8,4608]{1,0:T(8,128)(2,1)S(1)} %collective-permute-done.3.refs_3_), channel_id=1, source_target_pairs={{0,1},{1,0},{2,3},{3,2},{4,5},{5,4},{6,7},{7,6},{8,9},{9,8},{10,11... | collective-permute-start | bytes 221192 | tf_op jit(solution)/shard_map/ppermute | solution.py:248
  20.5 1.3 %collective-permute-start.12 = (bf16[8,4608]{1,0:T(8,128)(2,1)S(1)}, bf16[8,4608]{1,0:T(8,128)(2,1)S(1)}, u32[]{:S(2)}, u32[]{:S(2)}) collective-permute-start(bf16[8,4608]{1,0:T(8,128)(2,1)S(1)} %collective-permute-done.5.refs_5_), channel_id=1, source_target_pairs={{0,1},{1,0},{2,3},{3,2},{4,5},{5,4},{6,7},{7,6},{8,9},{9,8},{10,11... | collective-permute-start | bytes 221192 | tf_op jit(solution)/shard_map/ppermute | solution.py:248
  24.3 1.6 %collective-permute-start.15 = (bf16[32,4608]{1,0:T(8,128)(2,1)S(1)}, bf16[32,4608]{1,0:T(8,128)(2,1)S(1)}, u32[]{:S(2)}, u32[]{:S(2)}) collective-permute-start(bf16[32,4608]{1,0:T(8,128)(2,1)S(1)} %get-tuple-element.28), channel_id=1, source_target_pairs={{0,1},{1,0},{2,3},{3,2},{4,5},{5,4},{6,7},{7,6},{8,9},{9,8},{10,11... | collective-permute-start | bytes 884744 | tf_op jit(solution)/shard_map/ppermute | solution.py:248
  24.5 2.8 %collective-permute-start.19 = (bf16[32,4608]{1,0:T(8,128)(2,1)S(1)}, bf16[32,4608]{1,0:T(8,128)(2,1)S(1)}, u32[]{:S(2)}, u32[]{:S(2)}) collective-permute-start(bf16[32,4608]{1,0:T(8,128)(2,1)S(1)} %get-tuple-element.34), channel_id=1, source_target_pairs={{0,1},{1,0},{2,3},{3,2},{4,5},{5,4},{6,7},{7,6},{8,9},{9,8},{10,11... | collective-permute-start | bytes 884744 | tf_op jit(solution)/shard_map/ppermute | solution.py:248
  26.0 4.9 %collective-permute-start.17 = (bf16[8,4608]{1,0:T(8,128)(2,1)S(1)}, bf16[8,4608]{1,0:T(8,128)(2,1)S(1)}, u32[]{:S(2)}, u32[]{:S(2)}) collective-permute-start(bf16[8,4608]{1,0:T(8,128)(2,1)S(1)} %get-tuple-element.32), channel_id=1, source_target_pairs={{0,2},{1,3},{2,0},{3,1},{4,6},{5,7},{6,4},{7,5},{8,10},{9,11},{10,... | collective-permute-start | bytes 221192 | tf_op jit(solution)/shard_map/ppermute | solution.py:248
  27.4 5.2 %collective-permute-start.20 = (bf16[8,4608]{1,0:T(8,128)(2,1)S(1)}, bf16[8,4608]{1,0:T(8,128)(2,1)S(1)}, u32[]{:S(2)}, u32[]{:S(2)}) collective-permute-start(bf16[8,4608]{1,0:T(8,128)(2,1)S(1)} %get-tuple-element.36), channel_id=1, source_target_pairs={{0,2},{1,3},{2,0},{3,1},{4,6},{5,7},{6,4},{7,5},{8,10},{9,11},{10,... | collective-permute-start | bytes 221192 | tf_op jit(solution)/shard_map/ppermute | solution.py:248
  28.2 7.7 %collective-permute-start.22 = (bf16[8,4608]{1,0:T(8,128)(2,1)S(1)}, bf16[8,4608]{1,0:T(8,128)(2,1)S(1)}, u32[]{:S(2)}, u32[]{:S(2)}) collective-permute-start(bf16[8,4608]{1,0:T(8,128)(2,1)S(1)} %get-tuple-element.38), channel_id=1, source_target_pairs={{0,2},{1,3},{2,0},{3,1},{4,6},{5,7},{6,4},{7,5},{8,10},{9,11},{10,... | collective-permute-start | bytes 221192 | tf_op jit(solution)/shard_map/ppermute | solution.py:248
  29.5 7.9 %collective-permute-start.16 = (bf16[8,4608]{1,0:T(8,128)(2,1)S(1)}, bf16[8,4608]{1,0:T(8,128)(2,1)S(1)}, u32[]{:S(2)}, u32[]{:S(2)}) collective-permute-start(bf16[8,4608]{1,0:T(8,128)(2,1)S(1)} %get-tuple-element.30), channel_id=1, source_target_pairs={{0,2},{1,3},{2,0},{3,1},{4,6},{5,7},{6,4},{7,5},{8,10},{9,11},{10,... | collective-permute-start | bytes 221192 | tf_op jit(solution)/shard_map/ppermute | solution.py:248
  30.9 6.5 %collective-permute-start.18 = (bf16[8,4608]{1,0:T(8,128)(2,1)S(1)}, bf16[8,4608]{1,0:T(8,128)(2,1)S(1)}, u32[]{:S(2)}, u32[]{:S(2)}) collective-permute-start(bf16[8,4608]{1,0:T(8,128)(2,1)S(1)} %add.7), channel_id=1, source_target_pairs={{0,4},{1,5},{2,6},{3,7},{4,0},{5,1},{6,2},{7,3},{8,12},{9,13},{10,... | collective-permute-start | bytes 221192 | tf_op jit(solution)/shard_map/ppermute | solution.py:248
  32.6 7.9 %collective-permute-start.21 = (bf16[8,4608]{1,0:T(8,128)(2,1)S(1)}, bf16[8,4608]{1,0:T(8,128)(2,1)S(1)}, u32[]{:S(2)}, u32[]{:S(2)}) collective-permute-start(bf16[8,4608]{1,0:T(8,128)(2,1)S(1)} %add.9), channel_id=1, source_target_pairs={{0,8},{1,9},{2,10},{3,11},{4,12},{5,13},{6,14},{7,15},{8,0},{9,1},... | collective-permute-start | bytes 221192 | tf_op jit(solution)/shard_map/ppermute | solution.py:248
  36.0 6.2 %collective-permute-start.23 = (bf16[8,4608]{1,0:T(8,128)(2,1)S(1)}, bf16[8,4608]{1,0:T(8,128)(2,1)S(1)}, u32[]{:S(2)}, u32[]{:S(2)}) collective-permute-start(bf16[8,4608]{1,0:T(8,128)(2,1)S(1)} %add.10), channel_id=1, source_target_pairs={{0,12},{1,13},{2,14},{3,15},{4,8},{5,9},{6,10},{7,11},{8,4},{9,5},... | collective-permute-start | bytes 221192 | tf_op jit(solution)/shard_map/ppermute | solution.py:248
where the time goes:
time: 43.3 us; the launch traced here: 43.2 us
  starting transfers between devices  22.4 us (52%)
  waiting for transfers between devices  14.9 us (34%)
  Pallas kernels  5.13 us (12%)
  between operations  0.76 us (2%)
    ppermute x24, starting transfers between devices, swap(): lax.ppermute(value, 'expert', [(i, i ^ distance) for i in range(devices)])  22.4 us
    ppermute x24, waiting for transfers between devices, swap(): lax.ppermute(value, 'expert', [(i, i ^ distance) for i in range(devices)])  14.9 us
    pallas_call x1, Pallas kernels, ffn(): pl.pallas_call(functools.partial(ffn_kernel, len(pieces)), out_shape=[plt...  2.47 us
    pallas_call x1, Pallas kernels, pre(): pl.pallas_call(functools.partial(pre_kernel, experts), out_shape=[pltpu.V...  1.46 us
    pallas_call x1, Pallas kernels, combine(): pl.pallas_call(functools.partial(combine_kernel, experts), out_shape=jax....  1 us
  transfers between devices with their start and end apart: 24, of which 12 were waited for; matrix products, arithmetic and copies ran while one was open for 0% of the time, Pallas kernels for 0%

commit v1 on v0

--- a/solution.py
+++ b/solution.py
@@ -43,7 +43,7 @@
     return main, tail, blocks
 
 
-def pre_kernel(experts, z_ref, live_ref, ids_ref, tok_ref, gain_ref, router_ref, *outs):
+def pre_kernel(experts, members, ids_ref, tok_ref, gain_ref, router_ref, *outs):
     pieces, table_ref = outs[:-1], outs[-1]
     rows, width = tok_ref.shape
     main, tail, blocks = packing(width)
@@ -60,7 +60,6 @@
     for t in range(rows):
         first = jnp.where(row == t, ids_ref[0, t], first)
         second = jnp.where(row == t, ids_ref[1, t], second)
-    alive = row < live_ref[0]
     logits = [
         jnp.sum(normed_f32 * router_ref[e : e + 1, :].astype(F32), axis=-1, keepdims=True)
         for e in range(experts)
@@ -76,10 +75,10 @@
     r = lane % SUB
     k = (lane // SUB) % experts
     j = lane // (SUB * experts)
-    expert = k ^ z_ref[0]
+    expert = k ^ (lax.axis_index("expert") // members)
     is_first = first == expert
     is_second = second == expert
-    member = jnp.logical_and(jnp.logical_or(is_first, is_second), alive).astype(F32)
+    member = jnp.logical_or(is_first, is_second).astype(F32)
     slot = jnp.zeros((rows, lanes), F32)
     for t in range(rows - 1):
         slot = slot + jnp.where(row > t, member[t : t + 1, :], 0.0)
@@ -100,20 +99,20 @@
             piece[:, i * tail : (i + 1) * tail] = block[n * SUB : (n + 1) * SUB, :]
 
 
-def pre(tokens, norm_gain, router, expert_ids, live_rows, plane):
+def pre(tokens, norm_gain, router, expert_ids, members):
     rows, width = tokens.shape
     experts = router.shape[1]
     main, _, blocks = packing(width)
     lanes = (1 + blocks) * experts * SUB
     return pl.pallas_call(
-        functools.partial(pre_kernel, experts),
+        functools.partial(pre_kernel, experts, members),
         out_shape=[pltpu.VMEM((SUB, main), BF16)] * experts + [pltpu.VMEM((rows, lanes), F32)],
-        in_specs=[SMEM, SMEM, SMEM, VMEM, VMEM, VMEM],
+        in_specs=[SMEM, VMEM, VMEM, VMEM],
         out_specs=[VMEM] * (experts + 1),
         compiler_params=room(8),
         cost_estimate=pl.CostEstimate(flops=20 * 10**9, bytes_accessed=40 * 10**6, transcendentals=0),
         name="pre",
-    )(plane.reshape(1), live_rows, far(expert_ids.T), far(tokens), far(norm_gain.reshape(1, width)), far(router.T))
+    )(far(expert_ids.T), far(tokens), far(norm_gain.reshape(1, width)), far(router.T))
 
 
 def ffn_kernel(count, *refs):
@@ -202,13 +201,14 @@
     )(*map(near, terms))
 
 
-def combine_kernel(experts, table_ref, tok_ref, *refs):
+def combine_kernel(experts, live_ref, table_ref, tok_ref, *refs):
     pieces, out_ref = refs[:-1], refs[-1]
     own, others = pieces[: 1 - experts], [p[...] for p in pieces[1 - experts :]]
     width = tok_ref.shape[1]
     main, tail, blocks = packing(width)
     step = experts * SUB
-    table = table_ref[...]
+    row = lax.broadcasted_iota(jnp.int32, table_ref.shape, 0)
+    table = jnp.where(row < live_ref[0], table_ref[...], 0.0)
     high = table.astype(BF16)
     low = (table - high.astype(F32)).astype(BF16)
     first = own[0][...].astype(F32)
@@ -227,15 +227,15 @@
     out_ref[:, main:] = (tok_ref[:, main:].astype(F32) + rest).astype(BF16)
 
 
-def combine(experts, table, tokens, pieces):
+def combine(experts, live_rows, table, tokens, pieces):
     return pl.pallas_call(
         functools.partial(combine_kernel, experts),
         out_shape=jax.ShapeDtypeStruct(tokens.shape, BF16),
-        in_specs=[VMEM] * (2 + len(pieces)),
+        in_specs=[SMEM] + [VMEM] * (2 + len(pieces)),
         out_specs=VMEM,
         compiler_params=room(8),
         name="combine",
-    )(near(table), near(tokens), *map(near, pieces))
+    )(live_rows, near(table), near(tokens), *map(near, pieces))
 
 
 def local(tokens, norm_gain, router, w_gate, w_up, w_down, expert_ids, live_rows):
@@ -247,8 +247,7 @@
     def swap(value, distance):
         return lax.ppermute(value, "expert", [(i, i ^ distance) for i in range(devices)])
 
-    plane = lax.axis_index("expert") // members
-    *outgoing, table = pre(tokens, norm_gain, router, expert_ids, live_rows, plane)
+    *outgoing, table = pre(tokens, norm_gain, router, expert_ids, members)
     weights = [w_gate, w_up, w_down]
 
     here = {}
@@ -275,7 +274,7 @@
     for k in range(1, experts):
         (total,) = add(half[k], 1)
         home.append(swap(total, k * members))
-    return combine(experts, table, tokens, home)
+    return combine(experts, live_rows, table, tokens, home)
 
 
 def solution(mesh):

time: 43.3 us -> 39 us (0.901)
  waiting for transfers between devices: 14.9 us -> 11.1 us
    ppermute x24, waiting for transfers between devices: 14.9 us -> 11.1 us  [swap(): lax.ppermute(value, 'expert', [(i, i ^ distance) for i in range(devices)])]
    ppermute x24, starting transfers between devices: 22.4 us -> 22 us  [swap(): lax.ppermute(value, 'expert', [(i, i ^ distance) for i in range(devices)])]
  transfers between devices with their start and end apart: 24 -> 24, of which waited for: 12 -> 12; matrix products, arithmetic and copies ran while one was open for 0% -> 0% of each run, Pallas kernels for 0% -> 1%
where the time goes in v1:
time: 39 us; the launch traced here: 38.9 us
  starting transfers between devices  22 us (56%)
  waiting for transfers between devices  11.1 us (28%)
  Pallas kernels  5.14 us (13%)
  between operations  0.73 us (2%)
    ppermute x24, starting transfers between devices, swap(): lax.ppermute(value, 'expert', [(i, i ^ distance) for i in range(devices)])  22 us
    ppermute x24, waiting for transfers between devices, swap(): lax.ppermute(value, 'expert', [(i, i ^ distance) for i in range(devices)])  11.1 us
    pallas_call x1, Pallas kernels, ffn(): pl.pallas_call(functools.partial(ffn_kernel, len(pieces)), out_shape=[plt...  2.47 us
    pallas_call x1, Pallas kernels, pre(): pl.pallas_call(functools.partial(pre_kernel, experts, members), out_shape...  1.47 us
    pallas_call x1, Pallas kernels, combine(): pl.pallas_call(functools.partial(combine_kernel, experts), out_shape=jax....  1 us
  transfers between devices with their start and end apart: 24, of which 12 were waited for; matrix products, arithmetic and copies ran while one was open for 0% of the time, Pallas kernels for 1%

profile of v1, /device:TPU:0, one launch (start us, length us, event | category | flops | bytes accessed | tf_op | source)
XLA Modules:
  0.0 38.9 jit_solution(4054557450968425195)
XLA Ops:
  0.0 0.0 copy-start
  0.0 0.0 copy-start.1
  0.0 0.0 copy-start.2
  0.0 1.5 %pre.1 = (bf16[8,4608]{1,0:T(8,128)(2,1)S(1)}, bf16[8,4608]{1,0:T(8,128)(2,1)S(1)}, bf16[8,4608]{1,0:T(8,128)(2,1)S(1)}, bf16[8,4608]{1,0:T(8,128)(2,1)S(1)}, f32[8,128]{1,0:T(8,128)S(1)}) custom-call(s32[2,8]{1,0:T(2,128)} %bitcast.5, bf16[8,6144]{1,0:T(8,128)(2,1)} %tok_ref.3, f32[1,6144]{1,0:T(1,128)} %bitcast.4, bf16[4,6144]{1,0:T(4,128)(2,1)} %bitcast.3), custom_call_target="tpu_custom_call" | custom-call | flops 20000000000 | bytes 40000000 | tf_op jit(solution)/shard_map/pre/pallas_call | solution.py:107
  1.5 5.1 %collective-permute-start.2 = (bf16[8,4608]{1,0:T(8,128)(2,1)S(1)}, bf16[8,4608]{1,0:T(8,128)(2,1)S(1)}, u32[]{:S(2)}, u32[]{:S(2)}) collective-permute-start(bf16[8,4608]{1,0:T(8,128)(2,1)S(1)} %get-tuple-element.24), channel_id=1, source_target_pairs={{0,12},{1,13},{2,14},{3,15},{4,8},{5,9},{6,10},{7,11},{8,4},{9,5},... | collective-permute-start | bytes 221192 | tf_op jit(solution)/shard_map/ppermute | solution.py:248
  6.6 0.0 collective-permute-start.4
  6.6 0.6 %collective-permute-start = (bf16[8,4608]{1,0:T(8,128)(2,1)S(1)}, bf16[8,4608]{1,0:T(8,128)(2,1)S(1)}, u32[]{:S(2)}, u32[]{:S(2)}) collective-permute-start(bf16[8,4608]{1,0:T(8,128)(2,1)S(1)} %get-tuple-element.23), channel_id=1, source_target_pairs={{0,8},{1,9},{2,10},{3,11},{4,12},{5,13},{6,14},{7,15},{8,0},{9,1},... | collective-permute-start | bytes 221192 | tf_op jit(solution)/shard_map/ppermute | solution.py:248
  7.3 0.0 copy-start.3
  7.3 1.7 %collective-permute-start.6 = (bf16[8,4608]{1,0:T(8,128)(2,1)S(1)}, bf16[8,4608]{1,0:T(8,128)(2,1)S(1)}, u32[]{:S(2)}, u32[]{:S(2)}) collective-permute-start(bf16[8,4608]{1,0:T(8,128)(2,1)S(1)} %get-tuple-element.26.refs_6_), channel_id=1, source_target_pairs={{0,2},{1,3},{2,0},{3,1},{4,6},{5,7},{6,4},{7,5},{8,10},{9,11},{10,... | collective-permute-start | bytes 221192 | tf_op jit(solution)/shard_map/ppermute | solution.py:248
  8.9 0.0 collective-permute-start.13
  8.9 0.8 %collective-permute-done.2.refs_2_ = bf16[8,4608]{1,0:T(8,128)(2,1)S(1)} collective-permute-done((bf16[8,4608]{1,0:T(8,128)(2,1)S(1)}, bf16[8,4608]{1,0:T(8,128)(2,1)S(1)}, u32[]{:S(2)}, u32[]{:S(2)}) %collective-permute-start.2) | collective-permute-done | bytes 73760 | tf_op jit(solution)/shard_map/ppermute | solution.py:248
  9.8 1.5 %collective-permute-start.3 = (bf16[8,4608]{1,0:T(8,128)(2,1)S(1)}, bf16[8,4608]{1,0:T(8,128)(2,1)S(1)}, u32[]{:S(2)}, u32[]{:S(2)}) collective-permute-start(bf16[8,4608]{1,0:T(8,128)(2,1)S(1)} %collective-permute-done.2.refs_2_), channel_id=1, source_target_pairs={{0,2},{1,3},{2,0},{3,1},{4,6},{5,7},{6,4},{7,5},{8,10},{9,11},{10,... | collective-permute-start | bytes 221192 | tf_op jit(solution)/shard_map/ppermute | solution.py:248
  11.3 0.4 collective-permute-done.4.refs_4_
  11.7 1.6 %collective-permute-start.5 = (bf16[8,4608]{1,0:T(8,128)(2,1)S(1)}, bf16[8,4608]{1,0:T(8,128)(2,1)S(1)}, u32[]{:S(2)}, u32[]{:S(2)}) collective-permute-start(bf16[8,4608]{1,0:T(8,128)(2,1)S(1)} %collective-permute-done.4.refs_4_), channel_id=1, source_target_pairs={{0,2},{1,3},{2,0},{3,1},{4,6},{5,7},{6,4},{7,5},{8,10},{9,11},{10,... | collective-permute-start | bytes 221192 | tf_op jit(solution)/shard_map/ppermute | solution.py:248
  13.3 0.0 collective-permute-done.refs_0_
  13.3 0.7 %collective-permute-start.1 = (bf16[8,4608]{1,0:T(8,128)(2,1)S(1)}, bf16[8,4608]{1,0:T(8,128)(2,1)S(1)}, u32[]{:S(2)}, u32[]{:S(2)}) collective-permute-start(bf16[8,4608]{1,0:T(8,128)(2,1)S(1)} %collective-permute-done.refs_0_), channel_id=1, source_target_pairs={{0,2},{1,3},{2,0},{3,1},{4,6},{5,7},{6,4},{7,5},{8,10},{9,11},{10,... | collective-permute-start | bytes 221192 | tf_op jit(solution)/shard_map/ppermute | solution.py:248
  14.1 0.0 collective-permute-done.6.refs_7_
  14.1 0.0 collective-permute-start.14
  14.1 0.0 collective-permute-done.13.refs_14_
  14.1 0.5 %collective-permute-start.11 = (bf16[8,4608]{1,0:T(8,128)(2,1)S(1)}, bf16[8,4608]{1,0:T(8,128)(2,1)S(1)}, u32[]{:S(2)}, u32[]{:S(2)}) collective-permute-start(bf16[8,4608]{1,0:T(8,128)(2,1)S(1)} %collective-permute-done.4.refs_4_), channel_id=1, source_target_pairs={{0,1},{1,0},{2,3},{3,2},{4,5},{5,4},{6,7},{7,6},{8,9},{9,8},{10,11... | collective-permute-start | bytes 221192 | tf_op jit(solution)/shard_map/ppermute | solution.py:248
  14.6 0.0 collective-permute-done.3.refs_3_
  14.6 0.1 collective-permute-start.7
  14.6 2.1 %collective-permute-done.5.refs_5_ = bf16[8,4608]{1,0:T(8,128)(2,1)S(1)} collective-permute-done((bf16[8,4608]{1,0:T(8,128)(2,1)S(1)}, bf16[8,4608]{1,0:T(8,128)(2,1)S(1)}, u32[]{:S(2)}, u32[]{:S(2)}) %collective-permute-start.5) | collective-permute-done | bytes 73760 | tf_op jit(solution)/shard_map/ppermute | solution.py:248
  16.8 0.0 collective-permute-start.9
  16.8 0.9 %collective-permute-done.1.refs_1_ = bf16[8,4608]{1,0:T(8,128)(2,1)S(1)} collective-permute-done((bf16[8,4608]{1,0:T(8,128)(2,1)S(1)}, bf16[8,4608]{1,0:T(8,128)(2,1)S(1)}, u32[]{:S(2)}, u32[]{:S(2)}) %collective-permute-start.1) | collective-permute-done | bytes 73760 | tf_op jit(solution)/shard_map/ppermute | solution.py:248
  17.7 0.0 collective-permute-start.10
  17.7 0.0 collective-permute-done.14.refs_15_
  17.7 0.5 %collective-permute-start.12 = (bf16[8,4608]{1,0:T(8,128)(2,1)S(1)}, bf16[8,4608]{1,0:T(8,128)(2,1)S(1)}, u32[]{:S(2)}, u32[]{:S(2)}) collective-permute-start(bf16[8,4608]{1,0:T(8,128)(2,1)S(1)} %collective-permute-done.5.refs_5_), channel_id=1, source_target_pairs={{0,1},{1,0},{2,3},{3,2},{4,5},{5,4},{6,7},{7,6},{8,9},{9,8},{10,11... | collective-permute-start | bytes 221192 | tf_op jit(solution)/shard_map/ppermute | solution.py:248
  18.2 0.0 collective-permute-done.11.refs_12_
  18.2 0.1 collective-permute-start.8
  18.3 0.0 collective-permute-done.7.refs_8_
  18.3 0.0 collective-permute-done.9.refs_10_
  18.3 0.7 %collective-permute-done.10.refs_11_ = bf16[8,4608]{1,0:T(8,128)(2,1)S(1)} collective-permute-done((bf16[8,4608]{1,0:T(8,128)(2,1)S(1)}, bf16[8,4608]{1,0:T(8,128)(2,1)S(1)}, u32[]{:S(2)}, u32[]{:S(2)}) %collective-permute-start.10) | collective-permute-done | bytes 73760 | tf_op jit(solution)/shard_map/ppermute | solution.py:248
  19.0 0.2 collective-permute-done.12.refs_13_
  19.1 0.4 collective-permute-done.8.refs_9_
  19.5 0.0 copy-done
  19.5 0.0 copy-done.1
  19.5 0.0 copy-done.2
  19.5 2.5 %ffn.1 = (bf16[32,4608]{1,0:T(8,128)(2,1)S(1)}, bf16[32,4608]{1,0:T(8,128)(2,1)S(1)}, bf16[32,4608]{1,0:T(8,128)(2,1)S(1)}, bf16[32,4608]{1,0:T(8,128)(2,1)S(1)}) custom-call(bf16[8,4608]{1,0:T(8,128)(2,1)S(1)} %collective-permute-done.refs_0_, bf16[8,4608]{1,0:T(8,128)(2,1)S(1)} %collective-permute-done.1.refs_1_, ...), custom_call_target="tpu_custom_call" | custom-call | tf_op jit(solution)/shard_map/ffn/pallas_call | solution.py:170
  22.0 0.2 collective-permute-start.19
  22.2 0.4 collective-permute-start.15
  22.5 1.1 %collective-permute-done.19.refs_1_ = bf16[32,4608]{1,0:T(8,128)(2,1)S(1)} collective-permute-done((bf16[32,4608]{1,0:T(8,128)(2,1)S(1)}, bf16[32,4608]{1,0:T(8,128)(2,1)S(1)}, u32[]{:S(2)}, u32[]{:S(2)}) %collective-permute-start.19) | collective-permute-done | bytes 294944 | tf_op jit(solution)/shard_map/ppermute | solution.py:248
  23.6 0.1 add.7
  23.7 1.2 %collective-permute-start.22 = (bf16[8,4608]{1,0:T(8,128)(2,1)S(1)}, bf16[8,4608]{1,0:T(8,128)(2,1)S(1)}, u32[]{:S(2)}, u32[]{:S(2)}) collective-permute-start(bf16[8,4608]{1,0:T(8,128)(2,1)S(1)} %get-tuple-element.38), channel_id=1, source_target_pairs={{0,2},{1,3},{2,0},{3,1},{4,6},{5,7},{6,4},{7,5},{8,10},{9,11},{10,... | collective-permute-start | bytes 221192 | tf_op jit(solution)/shard_map/ppermute | solution.py:248
  24.9 0.9 %collective-permute-start.20 = (bf16[8,4608]{1,0:T(8,128)(2,1)S(1)}, bf16[8,4608]{1,0:T(8,128)(2,1)S(1)}, u32[]{:S(2)}, u32[]{:S(2)}) collective-permute-start(bf16[8,4608]{1,0:T(8,128)(2,1)S(1)} %get-tuple-element.36), channel_id=1, source_target_pairs={{0,2},{1,3},{2,0},{3,1},{4,6},{5,7},{6,4},{7,5},{8,10},{9,11},{10,... | collective-permute-start | bytes 221192 | tf_op jit(solution)/shard_map/ppermute | solution.py:248
  25.8 0.0 collective-permute-done.15.refs_1_
  25.8 0.1 add.5
  25.9 1.2 %collective-permute-start.17 = (bf16[8,4608]{1,0:T(8,128)(2,1)S(1)}, bf16[8,4608]{1,0:T(8,128)(2,1)S(1)}, u32[]{:S(2)}, u32[]{:S(2)}) collective-permute-start(bf16[8,4608]{1,0:T(8,128)(2,1)S(1)} %get-tuple-element.32), channel_id=1, source_target_pairs={{0,2},{1,3},{2,0},{3,1},{4,6},{5,7},{6,4},{7,5},{8,10},{9,11},{10,... | collective-permute-start | bytes 221192 | tf_op jit(solution)/shard_map/ppermute | solution.py:248
  27.1 0.9 %collective-permute-start.16 = (bf16[8,4608]{1,0:T(8,128)(2,1)S(1)}, bf16[8,4608]{1,0:T(8,128)(2,1)S(1)}, u32[]{:S(2)}, u32[]{:S(2)}) collective-permute-start(bf16[8,4608]{1,0:T(8,128)(2,1)S(1)} %get-tuple-element.30), channel_id=1, source_target_pairs={{0,2},{1,3},{2,0},{3,1},{4,6},{5,7},{6,4},{7,5},{8,10},{9,11},{10,... | collective-permute-start | bytes 221192 | tf_op jit(solution)/shard_map/ppermute | solution.py:248
  27.9 0.9 %collective-permute-done.22.refs_1_ = bf16[8,4608]{1,0:T(8,128)(2,1)S(1)} collective-permute-done((bf16[8,4608]{1,0:T(8,128)(2,1)S(1)}, bf16[8,4608]{1,0:T(8,128)(2,1)S(1)}, u32[]{:S(2)}, u32[]{:S(2)}) %collective-permute-start.22) | collective-permute-done | bytes 73760 | tf_op jit(solution)/shard_map/ppermute | solution.py:248
  28.9 2.7 %collective-permute-start.23 = (bf16[8,4608]{1,0:T(8,128)(2,1)S(1)}, bf16[8,4608]{1,0:T(8,128)(2,1)S(1)}, u32[]{:S(2)}, u32[]{:S(2)}) collective-permute-start(bf16[8,4608]{1,0:T(8,128)(2,1)S(1)} %add.9), channel_id=1, source_target_pairs={{0,12},{1,13},{2,14},{3,15},{4,8},{5,9},{6,10},{7,11},{8,4},{9,5},... | collective-permute-start | bytes 221192 | tf_op jit(solution)/shard_map/ppermute | solution.py:248
  31.5 0.0 collective-permute-done.20.refs_1_
  31.6 0.3 collective-permute-start.21
  31.9 0.1 collective-permute-done.17.refs_1_
  32.0 1.7 %collective-permute-start.18 = (bf16[8,4608]{1,0:T(8,128)(2,1)S(1)}, bf16[8,4608]{1,0:T(8,128)(2,1)S(1)}, u32[]{:S(2)}, u32[]{:S(2)}) collective-permute-start(bf16[8,4608]{1,0:T(8,128)(2,1)S(1)} %add.6), channel_id=1, source_target_pairs={{0,4},{1,5},{2,6},{3,7},{4,0},{5,1},{6,2},{7,3},{8,12},{9,13},{10,... | collective-permute-start | bytes 221192 | tf_op jit(solution)/shard_map/ppermute | solution.py:248
  34.4 0.0 collective-permute-done.16.refs_1_
  34.4 1.4 %collective-permute-done.23.refs_4_ = bf16[8,4608]{1,0:T(8,128)(2,1)S(1)} collective-permute-done((bf16[8,4608]{1,0:T(8,128)(2,1)S(1)}, bf16[8,4608]{1,0:T(8,128)(2,1)S(1)}, u32[]{:S(2)}, u32[]{:S(2)}) %collective-permute-start.23) | collective-permute-done | bytes 73760 | tf_op jit(solution)/shard_map/ppermute | solution.py:248
  35.8 2.1 %collective-permute-done.21.refs_3_ = bf16[8,4608]{1,0:T(8,128)(2,1)S(1)} collective-permute-done((bf16[8,4608]{1,0:T(8,128)(2,1)S(1)}, bf16[8,4608]{1,0:T(8,128)(2,1)S(1)}, u32[]{:S(2)}, u32[]{:S(2)}) %collective-permute-start.21) | collective-permute-done | bytes 73760 | tf_op jit(solution)/shard_map/ppermute | solution.py:248
  37.9 0.0 collective-permute-done.18.refs_2_
  37.9 0.0 copy-done.3
  37.9 1.0 %combine.1 = bf16[8,6144]{1,0:T(8,128)(2,1)} custom-call(s32[1]{0:T(128)S(6)} %copy.9.live_ref, f32[8,128]{1,0:T(8,128)S(1)} %get-tuple-element.22.table_ref, bf16[8,6144]{1,0:T(8,128)(2,1)S(1)} %copy-done.3, bf16[8,4608]{1,0:T(8,128)(2,1)S(1)} %get-tuple-element.29.refs_0_, bf16[8,4608]{1,0:T(8,128)(2,1)S(1)} %collective-permute-done.16.refs_1_, ...), custom_call_target="tpu_custom_call" | custom-call | tf_op jit(solution)/shard_map/combine/pallas_call | solution.py:231
  (3 shorter events, 0.1 us)
Async XLA Ops:
  0.0 19.5 %copy-start = (bf16[6144,256]{1,0:T(8,128)(2,1)S(1)}, bf16[6144,256]{1,0:T(8,128)(2,1)}, u32[]{:S(2)}) copy-start(bf16[6144,256]{1,0:T(8,128)(2,1)} %refs_16_.1) | copy-start | bytes 9437188
  0.0 19.5 %copy-start.1 = (bf16[6144,256]{1,0:T(8,128)(2,1)S(1)}, bf16[6144,256]{1,0:T(8,128)(2,1)}, u32[]{:S(2)}) copy-start(bf16[6144,256]{1,0:T(8,128)(2,1)} %refs_17_.1) | copy-start | bytes 9437188
  0.0 19.5 %copy-start.2 = (bf16[256,6144]{1,0:T(8,128)(2,1)S(1)}, bf16[256,6144]{1,0:T(8,128)(2,1)}, u32[]{:S(2)}) copy-start(bf16[256,6144]{1,0:T(8,128)(2,1)} %refs_18_.1) | copy-start | bytes 9437188
  1.5 8.3 %collective-permute-start.2 = (bf16[8,4608]{1,0:T(8,128)(2,1)S(1)}, bf16[8,4608]{1,0:T(8,128)(2,1)S(1)}, u32[]{:S(2)}, u32[]{:S(2)}) collective-permute-start(bf16[8,4608]{1,0:T(8,128)(2,1)S(1)} %get-tuple-element.24), channel_id=1, source_target_pairs={{0,12},{1,13},{2,14},{3,15},{4,8},{5,9},{6,10},{7,11},{8,4},{9,5},... | collective-permute-start | bytes 221192 | tf_op jit(solution)/shard_map/ppermute | solution.py:248
  6.6 5.1 %collective-permute-start.4 = (bf16[8,4608]{1,0:T(8,128)(2,1)S(1)}, bf16[8,4608]{1,0:T(8,128)(2,1)S(1)}, u32[]{:S(2)}, u32[]{:S(2)}) collective-permute-start(bf16[8,4608]{1,0:T(8,128)(2,1)S(1)} %get-tuple-element.25), channel_id=1, source_target_pairs={{0,4},{1,5},{2,6},{3,7},{4,0},{5,1},{6,2},{7,3},{8,12},{9,13},{10,... | collective-permute-start | bytes 221192 | tf_op jit(solution)/shard_map/ppermute | solution.py:248
  6.6 6.7 %collective-permute-start = (bf16[8,4608]{1,0:T(8,128)(2,1)S(1)}, bf16[8,4608]{1,0:T(8,128)(2,1)S(1)}, u32[]{:S(2)}, u32[]{:S(2)}) collective-permute-start(bf16[8,4608]{1,0:T(8,128)(2,1)S(1)} %get-tuple-element.23), channel_id=1, source_target_pairs={{0,8},{1,9},{2,10},{3,11},{4,12},{5,13},{6,14},{7,15},{8,0},{9,1},... | collective-permute-start | bytes 221192 | tf_op jit(solution)/shard_map/ppermute | solution.py:248
  7.3 30.6 %copy-start.3 = (bf16[8,6144]{1,0:T(8,128)(2,1)S(1)}, bf16[8,6144]{1,0:T(8,128)(2,1)}, u32[]{:S(2)}) copy-start(bf16[8,6144]{1,0:T(8,128)(2,1)} %tok_ref.3) | copy-start | bytes 294916
  7.3 6.8 %collective-permute-start.6 = (bf16[8,4608]{1,0:T(8,128)(2,1)S(1)}, bf16[8,4608]{1,0:T(8,128)(2,1)S(1)}, u32[]{:S(2)}, u32[]{:S(2)}) collective-permute-start(bf16[8,4608]{1,0:T(8,128)(2,1)S(1)} %get-tuple-element.26.refs_6_), channel_id=1, source_target_pairs={{0,2},{1,3},{2,0},{3,1},{4,6},{5,7},{6,4},{7,5},{8,10},{9,11},{10,... | collective-permute-start | bytes 221192 | tf_op jit(solution)/shard_map/ppermute | solution.py:248
  8.9 5.1 %collective-permute-start.13 = (bf16[8,4608]{1,0:T(8,128)(2,1)S(1)}, bf16[8,4608]{1,0:T(8,128)(2,1)S(1)}, u32[]{:S(2)}, u32[]{:S(2)}) collective-permute-start(bf16[8,4608]{1,0:T(8,128)(2,1)S(1)} %get-tuple-element.26.refs_6_), channel_id=1, source_target_pairs={{0,1},{1,0},{2,3},{3,2},{4,5},{5,4},{6,7},{7,6},{8,9},{9,8},{10,11... | collective-permute-start | bytes 221192 | tf_op jit(solution)/shard_map/ppermute | solution.py:248
  9.8 4.8 %collective-permute-start.3 = (bf16[8,4608]{1,0:T(8,128)(2,1)S(1)}, bf16[8,4608]{1,0:T(8,128)(2,1)S(1)}, u32[]{:S(2)}, u32[]{:S(2)}) collective-permute-start(bf16[8,4608]{1,0:T(8,128)(2,1)S(1)} %collective-permute-done.2.refs_2_), channel_id=1, source_target_pairs={{0,2},{1,3},{2,0},{3,1},{4,6},{5,7},{6,4},{7,5},{8,10},{9,11},{10,... | collective-permute-start | bytes 221192 | tf_op jit(solution)/shard_map/ppermute | solution.py:248
  11.7 5.1 %collective-permute-start.5 = (bf16[8,4608]{1,0:T(8,128)(2,1)S(1)}, bf16[8,4608]{1,0:T(8,128)(2,1)S(1)}, u32[]{:S(2)}, u32[]{:S(2)}) collective-permute-start(bf16[8,4608]{1,0:T(8,128)(2,1)S(1)} %collective-permute-done.4.refs_4_), channel_id=1, source_target_pairs={{0,2},{1,3},{2,0},{3,1},{4,6},{5,7},{6,4},{7,5},{8,10},{9,11},{10,... | collective-permute-start | bytes 221192 | tf_op jit(solution)/shard_map/ppermute | solution.py:248
  13.3 4.4 %collective-permute-start.1 = (bf16[8,4608]{1,0:T(8,128)(2,1)S(1)}, bf16[8,4608]{1,0:T(8,128)(2,1)S(1)}, u32[]{:S(2)}, u32[]{:S(2)}) collective-permute-start(bf16[8,4608]{1,0:T(8,128)(2,1)S(1)} %collective-permute-done.refs_0_), channel_id=1, source_target_pairs={{0,2},{1,3},{2,0},{3,1},{4,6},{5,7},{6,4},{7,5},{8,10},{9,11},{10,... | collective-permute-start | bytes 221192 | tf_op jit(solution)/shard_map/ppermute | solution.py:248
  14.1 3.6 %collective-permute-start.14 = (bf16[8,4608]{1,0:T(8,128)(2,1)S(1)}, bf16[8,4608]{1,0:T(8,128)(2,1)S(1)}, u32[]{:S(2)}, u32[]{:S(2)}) collective-permute-start(bf16[8,4608]{1,0:T(8,128)(2,1)S(1)} %collective-permute-done.6.refs_7_), channel_id=1, source_target_pairs={{0,1},{1,0},{2,3},{3,2},{4,5},{5,4},{6,7},{7,6},{8,9},{9,8},{10,11... | collective-permute-start | bytes 221192 | tf_op jit(solution)/shard_map/ppermute | solution.py:248
  14.1 4.1 %collective-permute-start.11 = (bf16[8,4608]{1,0:T(8,128)(2,1)S(1)}, bf16[8,4608]{1,0:T(8,128)(2,1)S(1)}, u32[]{:S(2)}, u32[]{:S(2)}) collective-permute-start(bf16[8,4608]{1,0:T(8,128)(2,1)S(1)} %collective-permute-done.4.refs_4_), channel_id=1, source_target_pairs={{0,1},{1,0},{2,3},{3,2},{4,5},{5,4},{6,7},{7,6},{8,9},{9,8},{10,11... | collective-permute-start | bytes 221192 | tf_op jit(solution)/shard_map/ppermute | solution.py:248
  14.6 3.7 %collective-permute-start.7 = (bf16[8,4608]{1,0:T(8,128)(2,1)S(1)}, bf16[8,4608]{1,0:T(8,128)(2,1)S(1)}, u32[]{:S(2)}, u32[]{:S(2)}) collective-permute-start(bf16[8,4608]{1,0:T(8,128)(2,1)S(1)} %collective-permute-done.refs_0_), channel_id=1, source_target_pairs={{0,1},{1,0},{2,3},{3,2},{4,5},{5,4},{6,7},{7,6},{8,9},{9,8},{10,11... | collective-permute-start | bytes 221192 | tf_op jit(solution)/shard_map/ppermute | solution.py:248
  16.8 1.5 %collective-permute-start.9 = (bf16[8,4608]{1,0:T(8,128)(2,1)S(1)}, bf16[8,4608]{1,0:T(8,128)(2,1)S(1)}, u32[]{:S(2)}, u32[]{:S(2)}) collective-permute-start(bf16[8,4608]{1,0:T(8,128)(2,1)S(1)} %collective-permute-done.2.refs_2_), channel_id=1, source_target_pairs={{0,1},{1,0},{2,3},{3,2},{4,5},{5,4},{6,7},{7,6},{8,9},{9,8},{10,11... | collective-permute-start | bytes 221192 | tf_op jit(solution)/shard_map/ppermute | solution.py:248
  17.7 1.3 %collective-permute-start.10 = (bf16[8,4608]{1,0:T(8,128)(2,1)S(1)}, bf16[8,4608]{1,0:T(8,128)(2,1)S(1)}, u32[]{:S(2)}, u32[]{:S(2)}) collective-permute-start(bf16[8,4608]{1,0:T(8,128)(2,1)S(1)} %collective-permute-done.3.refs_3_), channel_id=1, source_target_pairs={{0,1},{1,0},{2,3},{3,2},{4,5},{5,4},{6,7},{7,6},{8,9},{9,8},{10,11... | collective-permute-start | bytes 221192 | tf_op jit(solution)/shard_map/ppermute | solution.py:248
  17.7 1.4 %collective-permute-start.12 = (bf16[8,4608]{1,0:T(8,128)(2,1)S(1)}, bf16[8,4608]{1,0:T(8,128)(2,1)S(1)}, u32[]{:S(2)}, u32[]{:S(2)}) collective-permute-start(bf16[8,4608]{1,0:T(8,128)(2,1)S(1)} %collective-permute-done.5.refs_5_), channel_id=1, source_target_pairs={{0,1},{1,0},{2,3},{3,2},{4,5},{5,4},{6,7},{7,6},{8,9},{9,8},{10,11... | collective-permute-start | bytes 221192 | tf_op jit(solution)/shard_map/ppermute | solution.py:248
  18.2 1.3 %collective-permute-start.8 = (bf16[8,4608]{1,0:T(8,128)(2,1)S(1)}, bf16[8,4608]{1,0:T(8,128)(2,1)S(1)}, u32[]{:S(2)}, u32[]{:S(2)}) collective-permute-start(bf16[8,4608]{1,0:T(8,128)(2,1)S(1)} %collective-permute-done.1.refs_1_), channel_id=1, source_target_pairs={{0,1},{1,0},{2,3},{3,2},{4,5},{5,4},{6,7},{7,6},{8,9},{9,8},{10,11... | collective-permute-start | bytes 221192 | tf_op jit(solution)/shard_map/ppermute | solution.py:248
  22.0 1.6 %collective-permute-start.19 = (bf16[32,4608]{1,0:T(8,128)(2,1)S(1)}, bf16[32,4608]{1,0:T(8,128)(2,1)S(1)}, u32[]{:S(2)}, u32[]{:S(2)}) collective-permute-start(bf16[32,4608]{1,0:T(8,128)(2,1)S(1)} %get-tuple-element.34), channel_id=1, source_target_pairs={{0,1},{1,0},{2,3},{3,2},{4,5},{5,4},{6,7},{7,6},{8,9},{9,8},{10,11... | collective-permute-start | bytes 884744 | tf_op jit(solution)/shard_map/ppermute | solution.py:248
  22.2 3.6 %collective-permute-start.15 = (bf16[32,4608]{1,0:T(8,128)(2,1)S(1)}, bf16[32,4608]{1,0:T(8,128)(2,1)S(1)}, u32[]{:S(2)}, u32[]{:S(2)}) collective-permute-start(bf16[32,4608]{1,0:T(8,128)(2,1)S(1)} %get-tuple-element.28), channel_id=1, source_target_pairs={{0,1},{1,0},{2,3},{3,2},{4,5},{5,4},{6,7},{7,6},{8,9},{9,8},{10,11... | collective-permute-start | bytes 884744 | tf_op jit(solution)/shard_map/ppermute | solution.py:248
  23.7 5.2 %collective-permute-start.22 = (bf16[8,4608]{1,0:T(8,128)(2,1)S(1)}, bf16[8,4608]{1,0:T(8,128)(2,1)S(1)}, u32[]{:S(2)}, u32[]{:S(2)}) collective-permute-start(bf16[8,4608]{1,0:T(8,128)(2,1)S(1)} %get-tuple-element.38), channel_id=1, source_target_pairs={{0,2},{1,3},{2,0},{3,1},{4,6},{5,7},{6,4},{7,5},{8,10},{9,11},{10,... | collective-permute-start | bytes 221192 | tf_op jit(solution)/shard_map/ppermute | solution.py:248
  24.9 6.7 %collective-permute-start.20 = (bf16[8,4608]{1,0:T(8,128)(2,1)S(1)}, bf16[8,4608]{1,0:T(8,128)(2,1)S(1)}, u32[]{:S(2)}, u32[]{:S(2)}) collective-permute-start(bf16[8,4608]{1,0:T(8,128)(2,1)S(1)} %get-tuple-element.36), channel_id=1, source_target_pairs={{0,2},{1,3},{2,0},{3,1},{4,6},{5,7},{6,4},{7,5},{8,10},{9,11},{10,... | collective-permute-start | bytes 221192 | tf_op jit(solution)/shard_map/ppermute | solution.py:248
  25.9 6.2 %collective-permute-start.17 = (bf16[8,4608]{1,0:T(8,128)(2,1)S(1)}, bf16[8,4608]{1,0:T(8,128)(2,1)S(1)}, u32[]{:S(2)}, u32[]{:S(2)}) collective-permute-start(bf16[8,4608]{1,0:T(8,128)(2,1)S(1)} %get-tuple-element.32), channel_id=1, source_target_pairs={{0,2},{1,3},{2,0},{3,1},{4,6},{5,7},{6,4},{7,5},{8,10},{9,11},{10,... | collective-permute-start | bytes 221192 | tf_op jit(solution)/shard_map/ppermute | solution.py:248
  27.1 7.4 %collective-permute-start.16 = (bf16[8,4608]{1,0:T(8,128)(2,1)S(1)}, bf16[8,4608]{1,0:T(8,128)(2,1)S(1)}, u32[]{:S(2)}, u32[]{:S(2)}) collective-permute-start(bf16[8,4608]{1,0:T(8,128)(2,1)S(1)} %get-tuple-element.30), channel_id=1, source_target_pairs={{0,2},{1,3},{2,0},{3,1},{4,6},{5,7},{6,4},{7,5},{8,10},{9,11},{10,... | collective-permute-start | bytes 221192 | tf_op jit(solution)/shard_map/ppermute | solution.py:248
  28.9 6.9 %collective-permute-start.23 = (bf16[8,4608]{1,0:T(8,128)(2,1)S(1)}, bf16[8,4608]{1,0:T(8,128)(2,1)S(1)}, u32[]{:S(2)}, u32[]{:S(2)}) collective-permute-start(bf16[8,4608]{1,0:T(8,128)(2,1)S(1)} %add.9), channel_id=1, source_target_pairs={{0,12},{1,13},{2,14},{3,15},{4,8},{5,9},{6,10},{7,11},{8,4},{9,5},... | collective-permute-start | bytes 221192 | tf_op jit(solution)/shard_map/ppermute | solution.py:248
  31.6 6.3 %collective-permute-start.21 = (bf16[8,4608]{1,0:T(8,128)(2,1)S(1)}, bf16[8,4608]{1,0:T(8,128)(2,1)S(1)}, u32[]{:S(2)}, u32[]{:S(2)}) collective-permute-start(bf16[8,4608]{1,0:T(8,128)(2,1)S(1)} %add.8), channel_id=1, source_target_pairs={{0,8},{1,9},{2,10},{3,11},{4,12},{5,13},{6,14},{7,15},{8,0},{9,1},... | collective-permute-start | bytes 221192 | tf_op jit(solution)/shard_map/ppermute | solution.py:248
  32.0 5.9 %collective-permute-start.18 = (bf16[8,4608]{1,0:T(8,128)(2,1)S(1)}, bf16[8,4608]{1,0:T(8,128)(2,1)S(1)}, u32[]{:S(2)}, u32[]{:S(2)}) collective-permute-start(bf16[8,4608]{1,0:T(8,128)(2,1)S(1)} %add.6), channel_id=1, source_target_pairs={{0,4},{1,5},{2,6},{3,7},{4,0},{5,1},{6,2},{7,3},{8,12},{9,13},{10,... | collective-permute-start | bytes 221192 | tf_op jit(solution)/shard_map/ppermute | solution.py:248

commit v2 on v1

--- a/solution.py
+++ b/solution.py
@@ -83,7 +83,7 @@
     for t in range(rows - 1):
         slot = slot + jnp.where(row > t, member[t : t + 1, :], 0.0)
     main_slot = jnp.where(r < CAP, r, SUB)
-    tail_slot = jnp.where(r < CAP, SUB, (r - CAP) * blocks + j - 1)
+    tail_slot = jnp.where(r < CAP, SUB, (SUB - CAP) * (j - 1) + r - CAP)
     wanted = jnp.where(j == 0, main_slot, tail_slot).astype(F32)
     placed = jnp.where(slot == wanted, member, 0.0)
     gate = jnp.where(is_first, prob_first, prob_second)
@@ -119,40 +119,28 @@
     pieces = refs[:count]
     wg_ref, wu_ref, wd_ref = refs[count : count + 3]
     outs, x_ref = refs[count + 3 : -1], refs[-1]
-    width = wg_ref.shape[0]
-    hidden_width = wg_ref.shape[1]
+    total, width = x_ref.shape
     main, tail, blocks = packing(width)
+    spare = SUB - CAP
+    cuts = [slice(i * tail, (i + 1) * tail) for i in range(blocks)]
     at = 0
     for piece in pieces:
-        n = piece.shape[0]
-        x_ref[at : at + n, :] = piece[...]
-        at += n
-    total = at
+        for p in range(0, piece.shape[0], SUB):
+            x_ref[at : at + SUB, :main] = piece[p : p + SUB, :]
+            for i, cut in enumerate(cuts):
+                x_ref[at + spare * i : at + spare * (i + 1), main:] = piece[p + CAP : p + SUB, cut]
+            x_ref[at + CAP : at + SUB, main:] = jnp.zeros((spare, tail), BF16)
+            at += SUB
     size = 128 if total % 128 == 0 else total
-    row = lax.broadcasted_iota(jnp.int32, (size, size), 0)
-    col = lax.broadcasted_iota(jnp.int32, (size, size), 1)
-    same = row // SUB == col // SUB
-    in_row = lax.broadcasted_iota(jnp.int32, (size, hidden_width), 0) % SUB
 
     def chunk(base):
-        x = x_ref[pl.ds(base, size), :]
-        rest = jnp.zeros((size, tail), F32)
-        for i in range(blocks):
-            take = jnp.logical_and(same, row % SUB == (col % SUB - CAP) * blocks + i)
-            take = jnp.logical_and(take, col % SUB >= CAP)
-            rest = rest + dot(take.astype(BF16), x[:, i * tail : (i + 1) * tail])
-        rest = rest.astype(BF16)
-        gate = dot(x, wg_ref[:main, :]) + dot(rest, wg_ref[main:, :])
-        up = dot(x, wu_ref[:main, :]) + dot(rest, wu_ref[main:, :])
+        rows = pl.ds(base, size)
+        x = x_ref[rows, :]
+        gate = dot(x, wg_ref[...])
+        up = dot(x, wu_ref[...])
         hidden = (gate / (1.0 + jnp.exp(-gate)) * up).astype(BF16)
-        upper = jnp.where(in_row < CAP, hidden, jnp.zeros_like(hidden))
-        for i in range(blocks):
-            give = jnp.logical_and(same, col % SUB == (row % SUB - CAP) * blocks + i)
-            give = jnp.logical_and(give, row % SUB >= CAP)
-            lower = dot(give.astype(BF16), hidden).astype(BF16)
-            cols = slice(i * tail, (i + 1) * tail)
-            out = (dot(upper, wd_ref[:, cols]) + dot(lower, wd_ref[:, main:])).astype(BF16)
-            x_ref[pl.ds(base, size), cols] = out
+        for cut in cuts + [slice(main, width)]:
+            x_ref[rows, cut] = dot(hidden, wd_ref[:, cut]).astype(BF16)
 
     if total == size:
         chunk(0)
@@ -160,20 +148,22 @@
         lax.fori_loop(0, total // size, lambda n, c: (chunk(pl.multiple_of(n * size, size)), c)[1], 0)
     at = 0
     for out in outs:
-        n = out.shape[0]
-        out[...] = x_ref[at : at + n, :]
-        at += n
+        for p in range(0, out.shape[0], SUB):
+            out[p : p + SUB, :] = x_ref[at : at + SUB, :main]
+            for i, cut in enumerate(cuts):
+                out[p + CAP : p + SUB, cut] = x_ref[at + spare * i : at + spare * (i + 1), main:]
+            at += SUB
 
 
 def ffn(pieces, weights, sizes):
-    total, main = sum(sizes), pieces[0].shape[1]
+    total, main, width = sum(sizes), pieces[0].shape[1], weights[0].shape[0]
     return pl.pallas_call(
         functools.partial(ffn_kernel, len(pieces)),
         out_shape=[pltpu.VMEM((n, main), BF16) for n in sizes],
         in_specs=[VMEM] * (len(pieces) + 3),
         out_specs=[VMEM] * len(sizes),
-        scratch_shapes=[pltpu.VMEM((total, main), BF16)],
-        compiler_params=room(16),
+        scratch_shapes=[pltpu.VMEM((total, width), BF16)],
+        compiler_params=room(24),
         name="ffn",
     )(*map(near, pieces), *map(near, weights))
 
@@ -215,16 +205,17 @@
     for ref in own[1:]:
         first = first + ref[...].astype(F32)
     arrived = [first.astype(BF16)] + others
-    rest = jnp.zeros((tok_ref.shape[0], tail), F32)
+    rows = tok_ref.shape[0]
+    rest = tok_ref[:, main:].astype(F32)
     for i in range(blocks):
         cols = slice(i * tail, (i + 1) * tail)
         data = jnp.concatenate([p[:, cols] for p in arrived], axis=0)
         mine, theirs = slice(0, step), slice((1 + i) * step, (2 + i) * step)
-        out_ref[:, cols] = (
-            tok_ref[:, cols].astype(F32) + dot(high[:, mine], data) + dot(low[:, mine], data)
-        ).astype(BF16)
-        rest = rest + dot(high[:, theirs], data) + dot(low[:, theirs], data)
-    out_ref[:, main:] = (tok_ref[:, main:].astype(F32) + rest).astype(BF16)
+        sums = dot(jnp.concatenate([high[:, mine], low[:, mine], high[:, theirs], low[:, theirs]], axis=0), data)
+        parts = [sums[n * rows : (n + 1) * rows, :] for n in range(4)]
+        out_ref[:, cols] = (tok_ref[:, cols].astype(F32) + (parts[0] + parts[1])).astype(BF16)
+        rest = rest + (parts[2] + parts[3])
+    out_ref[:, main:] = rest.astype(BF16)
 
 
 def combine(experts, live_rows, table, tokens, pieces):

time: 39 us -> 38.2 us (0.979)
  Pallas kernels: 5.14 us -> 4.28 us
    pallas_call x1, Pallas kernels: 2.47 us -> 1.68 us  [ffn(): pl.pallas_call(functools.partial(ffn_kernel, len(pieces)), out_shape=[plt...]
where the time goes in v2:
time: 38.2 us; the launch traced here: 38.1 us
  starting transfers between devices  21.9 us (57%)
  waiting for transfers between devices  11.1 us (29%)
  Pallas kernels  4.28 us (11%)
  between operations  0.72 us (2%)
    ppermute x24, starting transfers between devices, swap(): lax.ppermute(value, 'expert', [(i, i ^ distance) for i in range(devices)])  21.9 us
    ppermute x24, waiting for transfers between devices, swap(): lax.ppermute(value, 'expert', [(i, i ^ distance) for i in range(devices)])  11.1 us
    pallas_call x1, Pallas kernels, ffn(): pl.pallas_call(functools.partial(ffn_kernel, len(pieces)), out_shape=[plt...  1.68 us
    pallas_call x1, Pallas kernels, pre(): pl.pallas_call(functools.partial(pre_kernel, experts, members), out_shape...  1.47 us
    pallas_call x1, Pallas kernels, combine(): pl.pallas_call(functools.partial(combine_kernel, experts), out_shape=jax....  0.93 us
  transfers between devices with their start and end apart: 24, of which 12 were waited for; matrix products, arithmetic and copies ran while one was open for 0% of the time, Pallas kernels for 1%

profile of v2, /device:TPU:0, one launch (start us, length us, event | category | flops | bytes accessed | tf_op | source)
XLA Modules:
  0.0 38.1 jit_solution(11945439076485048792)
XLA Ops:
  0.0 0.0 copy-start
  0.0 0.0 copy-start.1
  0.0 0.0 copy-start.2
  0.0 1.5 %pre.1 = (bf16[8,4608]{1,0:T(8,128)(2,1)S(1)}, bf16[8,4608]{1,0:T(8,128)(2,1)S(1)}, bf16[8,4608]{1,0:T(8,128)(2,1)S(1)}, bf16[8,4608]{1,0:T(8,128)(2,1)S(1)}, f32[8,128]{1,0:T(8,128)S(1)}) custom-call(s32[2,8]{1,0:T(2,128)} %bitcast.5, bf16[8,6144]{1,0:T(8,128)(2,1)} %tok_ref.3, f32[1,6144]{1,0:T(1,128)} %bitcast.4, bf16[4,6144]{1,0:T(4,128)(2,1)} %bitcast.3), custom_call_target="tpu_custom_call" | custom-call | flops 20000000000 | bytes 40000000 | tf_op jit(solution)/shard_map/pre/pallas_call | solution.py:107
  1.5 5.1 %collective-permute-start.2 = (bf16[8,4608]{1,0:T(8,128)(2,1)S(1)}, bf16[8,4608]{1,0:T(8,128)(2,1)S(1)}, u32[]{:S(2)}, u32[]{:S(2)}) collective-permute-start(bf16[8,4608]{1,0:T(8,128)(2,1)S(1)} %get-tuple-element.24), channel_id=1, source_target_pairs={{0,12},{1,13},{2,14},{3,15},{4,8},{5,9},{6,10},{7,11},{8,4},{9,5},... | collective-permute-start | bytes 221192 | tf_op jit(solution)/shard_map/ppermute | solution.py:239
  6.6 0.0 collective-permute-start.4
  6.6 0.6 %collective-permute-start = (bf16[8,4608]{1,0:T(8,128)(2,1)S(1)}, bf16[8,4608]{1,0:T(8,128)(2,1)S(1)}, u32[]{:S(2)}, u32[]{:S(2)}) collective-permute-start(bf16[8,4608]{1,0:T(8,128)(2,1)S(1)} %get-tuple-element.23), channel_id=1, source_target_pairs={{0,8},{1,9},{2,10},{3,11},{4,12},{5,13},{6,14},{7,15},{8,0},{9,1},... | collective-permute-start | bytes 221192 | tf_op jit(solution)/shard_map/ppermute | solution.py:239
  7.3 0.0 copy-start.3
  7.3 1.7 %collective-permute-start.6 = (bf16[8,4608]{1,0:T(8,128)(2,1)S(1)}, bf16[8,4608]{1,0:T(8,128)(2,1)S(1)}, u32[]{:S(2)}, u32[]{:S(2)}) collective-permute-start(bf16[8,4608]{1,0:T(8,128)(2,1)S(1)} %get-tuple-element.26.refs_6_), channel_id=1, source_target_pairs={{0,2},{1,3},{2,0},{3,1},{4,6},{5,7},{6,4},{7,5},{8,10},{9,11},{10,... | collective-permute-start | bytes 221192 | tf_op jit(solution)/shard_map/ppermute | solution.py:239
  8.9 0.0 collective-permute-start.13
  8.9 0.8 %collective-permute-done.2.refs_2_ = bf16[8,4608]{1,0:T(8,128)(2,1)S(1)} collective-permute-done((bf16[8,4608]{1,0:T(8,128)(2,1)S(1)}, bf16[8,4608]{1,0:T(8,128)(2,1)S(1)}, u32[]{:S(2)}, u32[]{:S(2)}) %collective-permute-start.2) | collective-permute-done | bytes 73760 | tf_op jit(solution)/shard_map/ppermute | solution.py:239
  9.8 1.5 %collective-permute-start.3 = (bf16[8,4608]{1,0:T(8,128)(2,1)S(1)}, bf16[8,4608]{1,0:T(8,128)(2,1)S(1)}, u32[]{:S(2)}, u32[]{:S(2)}) collective-permute-start(bf16[8,4608]{1,0:T(8,128)(2,1)S(1)} %collective-permute-done.2.refs_2_), channel_id=1, source_target_pairs={{0,2},{1,3},{2,0},{3,1},{4,6},{5,7},{6,4},{7,5},{8,10},{9,11},{10,... | collective-permute-start | bytes 221192 | tf_op jit(solution)/shard_map/ppermute | solution.py:239
  11.3 0.4 %collective-permute-done.4.refs_4_ = bf16[8,4608]{1,0:T(8,128)(2,1)S(1)} collective-permute-done((bf16[8,4608]{1,0:T(8,128)(2,1)S(1)}, bf16[8,4608]{1,0:T(8,128)(2,1)S(1)}, u32[]{:S(2)}, u32[]{:S(2)}) %collective-permute-start.4) | collective-permute-done | bytes 73760 | tf_op jit(solution)/shard_map/ppermute | solution.py:239
  11.7 1.6 %collective-permute-start.5 = (bf16[8,4608]{1,0:T(8,128)(2,1)S(1)}, bf16[8,4608]{1,0:T(8,128)(2,1)S(1)}, u32[]{:S(2)}, u32[]{:S(2)}) collective-permute-start(bf16[8,4608]{1,0:T(8,128)(2,1)S(1)} %collective-permute-done.4.refs_4_), channel_id=1, source_target_pairs={{0,2},{1,3},{2,0},{3,1},{4,6},{5,7},{6,4},{7,5},{8,10},{9,11},{10,... | collective-permute-start | bytes 221192 | tf_op jit(solution)/shard_map/ppermute | solution.py:239
  13.3 0.0 collective-permute-done.refs_0_
  13.3 0.7 %collective-permute-start.1 = (bf16[8,4608]{1,0:T(8,128)(2,1)S(1)}, bf16[8,4608]{1,0:T(8,128)(2,1)S(1)}, u32[]{:S(2)}, u32[]{:S(2)}) collective-permute-start(bf16[8,4608]{1,0:T(8,128)(2,1)S(1)} %collective-permute-done.refs_0_), channel_id=1, source_target_pairs={{0,2},{1,3},{2,0},{3,1},{4,6},{5,7},{6,4},{7,5},{8,10},{9,11},{10,... | collective-permute-start | bytes 221192 | tf_op jit(solution)/shard_map/ppermute | solution.py:239
  14.1 0.0 collective-permute-done.6.refs_7_
  14.1 0.0 collective-permute-start.14
  14.1 0.0 collective-permute-done.13.refs_14_
  14.1 0.5 %collective-permute-start.11 = (bf16[8,4608]{1,0:T(8,128)(2,1)S(1)}, bf16[8,4608]{1,0:T(8,128)(2,1)S(1)}, u32[]{:S(2)}, u32[]{:S(2)}) collective-permute-start(bf16[8,4608]{1,0:T(8,128)(2,1)S(1)} %collective-permute-done.4.refs_4_), channel_id=1, source_target_pairs={{0,1},{1,0},{2,3},{3,2},{4,5},{5,4},{6,7},{7,6},{8,9},{9,8},{10,11... | collective-permute-start | bytes 221192 | tf_op jit(solution)/shard_map/ppermute | solution.py:239
  14.6 0.0 collective-permute-done.3.refs_3_
  14.6 0.1 collective-permute-start.7
  14.6 2.1 %collective-permute-done.5.refs_5_ = bf16[8,4608]{1,0:T(8,128)(2,1)S(1)} collective-permute-done((bf16[8,4608]{1,0:T(8,128)(2,1)S(1)}, bf16[8,4608]{1,0:T(8,128)(2,1)S(1)}, u32[]{:S(2)}, u32[]{:S(2)}) %collective-permute-start.5) | collective-permute-done | bytes 73760 | tf_op jit(solution)/shard_map/ppermute | solution.py:239
  16.8 0.0 collective-permute-start.9
  16.8 0.9 %collective-permute-done.1.refs_1_ = bf16[8,4608]{1,0:T(8,128)(2,1)S(1)} collective-permute-done((bf16[8,4608]{1,0:T(8,128)(2,1)S(1)}, bf16[8,4608]{1,0:T(8,128)(2,1)S(1)}, u32[]{:S(2)}, u32[]{:S(2)}) %collective-permute-start.1) | collective-permute-done | bytes 73760 | tf_op jit(solution)/shard_map/ppermute | solution.py:239
  17.7 0.0 collective-permute-start.10
  17.7 0.0 collective-permute-done.14.refs_15_
  17.7 0.5 %collective-permute-start.12 = (bf16[8,4608]{1,0:T(8,128)(2,1)S(1)}, bf16[8,4608]{1,0:T(8,128)(2,1)S(1)}, u32[]{:S(2)}, u32[]{:S(2)}) collective-permute-start(bf16[8,4608]{1,0:T(8,128)(2,1)S(1)} %collective-permute-done.5.refs_5_), channel_id=1, source_target_pairs={{0,1},{1,0},{2,3},{3,2},{4,5},{5,4},{6,7},{7,6},{8,9},{9,8},{10,11... | collective-permute-start | bytes 221192 | tf_op jit(solution)/shard_map/ppermute | solution.py:239
  18.2 0.0 collective-permute-done.11.refs_12_
  18.2 0.1 collective-permute-start.8
  18.3 0.0 collective-permute-done.7.refs_8_
  18.3 0.0 collective-permute-done.9.refs_10_
  18.3 0.7 %collective-permute-done.10.refs_11_ = bf16[8,4608]{1,0:T(8,128)(2,1)S(1)} collective-permute-done((bf16[8,4608]{1,0:T(8,128)(2,1)S(1)}, bf16[8,4608]{1,0:T(8,128)(2,1)S(1)}, u32[]{:S(2)}, u32[]{:S(2)}) %collective-permute-start.10) | collective-permute-done | bytes 73760 | tf_op jit(solution)/shard_map/ppermute | solution.py:239
  19.0 0.2 collective-permute-done.12.refs_13_
  19.1 0.4 collective-permute-done.8.refs_9_
  19.5 0.0 copy-done
  19.5 0.0 copy-done.1
  19.5 0.0 copy-done.2
  19.5 1.7 %ffn.1 = (bf16[32,4608]{1,0:T(8,128)(2,1)S(1)}, bf16[32,4608]{1,0:T(8,128)(2,1)S(1)}, bf16[32,4608]{1,0:T(8,128)(2,1)S(1)}, bf16[32,4608]{1,0:T(8,128)(2,1)S(1)}) custom-call(bf16[8,4608]{1,0:T(8,128)(2,1)S(1)} %collective-permute-done.refs_0_, bf16[8,4608]{1,0:T(8,128)(2,1)S(1)} %collective-permute-done.1.refs_1_, ...), custom_call_target="tpu_custom_call" | custom-call | tf_op jit(solution)/shard_map/ffn/pallas_call | solution.py:160
  21.2 0.2 collective-permute-start.19
  21.4 0.4 collective-permute-start.15
  21.8 1.1 %collective-permute-done.19.refs_1_ = bf16[32,4608]{1,0:T(8,128)(2,1)S(1)} collective-permute-done((bf16[32,4608]{1,0:T(8,128)(2,1)S(1)}, bf16[32,4608]{1,0:T(8,128)(2,1)S(1)}, u32[]{:S(2)}, u32[]{:S(2)}) %collective-permute-start.19) | collective-permute-done | bytes 294944 | tf_op jit(solution)/shard_map/ppermute | solution.py:239
  22.8 0.1 add.7
  22.9 1.2 %collective-permute-start.22 = (bf16[8,4608]{1,0:T(8,128)(2,1)S(1)}, bf16[8,4608]{1,0:T(8,128)(2,1)S(1)}, u32[]{:S(2)}, u32[]{:S(2)}) collective-permute-start(bf16[8,4608]{1,0:T(8,128)(2,1)S(1)} %get-tuple-element.38), channel_id=1, source_target_pairs={{0,2},{1,3},{2,0},{3,1},{4,6},{5,7},{6,4},{7,5},{8,10},{9,11},{10,... | collective-permute-start | bytes 221192 | tf_op jit(solution)/shard_map/ppermute | solution.py:239
  24.1 0.9 %collective-permute-start.20 = (bf16[8,4608]{1,0:T(8,128)(2,1)S(1)}, bf16[8,4608]{1,0:T(8,128)(2,1)S(1)}, u32[]{:S(2)}, u32[]{:S(2)}) collective-permute-start(bf16[8,4608]{1,0:T(8,128)(2,1)S(1)} %get-tuple-element.36), channel_id=1, source_target_pairs={{0,2},{1,3},{2,0},{3,1},{4,6},{5,7},{6,4},{7,5},{8,10},{9,11},{10,... | collective-permute-start | bytes 221192 | tf_op jit(solution)/shard_map/ppermute | solution.py:239
  25.0 0.0 collective-permute-done.15.refs_1_
  25.0 0.1 add.5
  25.1 1.2 %collective-permute-start.17 = (bf16[8,4608]{1,0:T(8,128)(2,1)S(1)}, bf16[8,4608]{1,0:T(8,128)(2,1)S(1)}, u32[]{:S(2)}, u32[]{:S(2)}) collective-permute-start(bf16[8,4608]{1,0:T(8,128)(2,1)S(1)} %get-tuple-element.32), channel_id=1, source_target_pairs={{0,2},{1,3},{2,0},{3,1},{4,6},{5,7},{6,4},{7,5},{8,10},{9,11},{10,... | collective-permute-start | bytes 221192 | tf_op jit(solution)/shard_map/ppermute | solution.py:239
  26.3 0.9 %collective-permute-start.16 = (bf16[8,4608]{1,0:T(8,128)(2,1)S(1)}, bf16[8,4608]{1,0:T(8,128)(2,1)S(1)}, u32[]{:S(2)}, u32[]{:S(2)}) collective-permute-start(bf16[8,4608]{1,0:T(8,128)(2,1)S(1)} %get-tuple-element.30), channel_id=1, source_target_pairs={{0,2},{1,3},{2,0},{3,1},{4,6},{5,7},{6,4},{7,5},{8,10},{9,11},{10,... | collective-permute-start | bytes 221192 | tf_op jit(solution)/shard_map/ppermute | solution.py:239
  27.2 0.9 %collective-permute-done.22.refs_1_ = bf16[8,4608]{1,0:T(8,128)(2,1)S(1)} collective-permute-done((bf16[8,4608]{1,0:T(8,128)(2,1)S(1)}, bf16[8,4608]{1,0:T(8,128)(2,1)S(1)}, u32[]{:S(2)}, u32[]{:S(2)}) %collective-permute-start.22) | collective-permute-done | bytes 73760 | tf_op jit(solution)/shard_map/ppermute | solution.py:239
  28.1 2.7 %collective-permute-start.23 = (bf16[8,4608]{1,0:T(8,128)(2,1)S(1)}, bf16[8,4608]{1,0:T(8,128)(2,1)S(1)}, u32[]{:S(2)}, u32[]{:S(2)}) collective-permute-start(bf16[8,4608]{1,0:T(8,128)(2,1)S(1)} %add.9), channel_id=1, source_target_pairs={{0,12},{1,13},{2,14},{3,15},{4,8},{5,9},{6,10},{7,11},{8,4},{9,5},... | collective-permute-start | bytes 221192 | tf_op jit(solution)/shard_map/ppermute | solution.py:239
  30.8 0.0 collective-permute-done.20.refs_1_
  30.8 0.3 collective-permute-start.21
  31.1 0.2 collective-permute-done.17.refs_1_
  31.3 1.7 %collective-permute-start.18 = (bf16[8,4608]{1,0:T(8,128)(2,1)S(1)}, bf16[8,4608]{1,0:T(8,128)(2,1)S(1)}, u32[]{:S(2)}, u32[]{:S(2)}) collective-permute-start(bf16[8,4608]{1,0:T(8,128)(2,1)S(1)} %add.6), channel_id=1, source_target_pairs={{0,4},{1,5},{2,6},{3,7},{4,0},{5,1},{6,2},{7,3},{8,12},{9,13},{10,... | collective-permute-start | bytes 221192 | tf_op jit(solution)/shard_map/ppermute | solution.py:239
  33.6 0.0 collective-permute-done.16.refs_1_
  33.7 1.4 %collective-permute-done.23.refs_4_ = bf16[8,4608]{1,0:T(8,128)(2,1)S(1)} collective-permute-done((bf16[8,4608]{1,0:T(8,128)(2,1)S(1)}, bf16[8,4608]{1,0:T(8,128)(2,1)S(1)}, u32[]{:S(2)}, u32[]{:S(2)}) %collective-permute-start.23) | collective-permute-done | bytes 73760 | tf_op jit(solution)/shard_map/ppermute | solution.py:239
  35.0 2.1 %collective-permute-done.21.refs_3_ = bf16[8,4608]{1,0:T(8,128)(2,1)S(1)} collective-permute-done((bf16[8,4608]{1,0:T(8,128)(2,1)S(1)}, bf16[8,4608]{1,0:T(8,128)(2,1)S(1)}, u32[]{:S(2)}, u32[]{:S(2)}) %collective-permute-start.21) | collective-permute-done | bytes 73760 | tf_op jit(solution)/shard_map/ppermute | solution.py:239
  37.1 0.0 collective-permute-done.18.refs_2_
  37.1 0.0 copy-done.3
  37.1 0.9 %combine.1 = bf16[8,6144]{1,0:T(8,128)(2,1)} custom-call(s32[1]{0:T(128)S(6)} %copy.9.live_ref, f32[8,128]{1,0:T(8,128)S(1)} %get-tuple-element.22.table_ref, bf16[8,6144]{1,0:T(8,128)(2,1)S(1)} %copy-done.3, bf16[8,4608]{1,0:T(8,128)(2,1)S(1)} %get-tuple-element.29.refs_0_, bf16[8,4608]{1,0:T(8,128)(2,1)S(1)} %collective-permute-done.16.refs_1_, ...), custom_call_target="tpu_custom_call" | custom-call | tf_op jit(solution)/shard_map/combine/pallas_call | solution.py:222
  (3 shorter events, 0.1 us)
Async XLA Ops:
  0.0 19.5 %copy-start = (bf16[6144,256]{1,0:T(8,128)(2,1)S(1)}, bf16[6144,256]{1,0:T(8,128)(2,1)}, u32[]{:S(2)}) copy-start(bf16[6144,256]{1,0:T(8,128)(2,1)} %refs_16_.1) | copy-start | bytes 9437188
  0.0 19.5 %copy-start.1 = (bf16[6144,256]{1,0:T(8,128)(2,1)S(1)}, bf16[6144,256]{1,0:T(8,128)(2,1)}, u32[]{:S(2)}) copy-start(bf16[6144,256]{1,0:T(8,128)(2,1)} %refs_17_.1) | copy-start | bytes 9437188
  0.0 19.5 %copy-start.2 = (bf16[256,6144]{1,0:T(8,128)(2,1)S(1)}, bf16[256,6144]{1,0:T(8,128)(2,1)}, u32[]{:S(2)}) copy-start(bf16[256,6144]{1,0:T(8,128)(2,1)} %refs_18_.1) | copy-start | bytes 9437188
  1.5 8.3 %collective-permute-start.2 = (bf16[8,4608]{1,0:T(8,128)(2,1)S(1)}, bf16[8,4608]{1,0:T(8,128)(2,1)S(1)}, u32[]{:S(2)}, u32[]{:S(2)}) collective-permute-start(bf16[8,4608]{1,0:T(8,128)(2,1)S(1)} %get-tuple-element.24), channel_id=1, source_target_pairs={{0,12},{1,13},{2,14},{3,15},{4,8},{5,9},{6,10},{7,11},{8,4},{9,5},... | collective-permute-start | bytes 221192 | tf_op jit(solution)/shard_map/ppermute | solution.py:239
  6.6 5.1 %collective-permute-start.4 = (bf16[8,4608]{1,0:T(8,128)(2,1)S(1)}, bf16[8,4608]{1,0:T(8,128)(2,1)S(1)}, u32[]{:S(2)}, u32[]{:S(2)}) collective-permute-start(bf16[8,4608]{1,0:T(8,128)(2,1)S(1)} %get-tuple-element.25), channel_id=1, source_target_pairs={{0,4},{1,5},{2,6},{3,7},{4,0},{5,1},{6,2},{7,3},{8,12},{9,13},{10,... | collective-permute-start | bytes 221192 | tf_op jit(solution)/shard_map/ppermute | solution.py:239
  6.6 6.7 %collective-permute-start = (bf16[8,4608]{1,0:T(8,128)(2,1)S(1)}, bf16[8,4608]{1,0:T(8,128)(2,1)S(1)}, u32[]{:S(2)}, u32[]{:S(2)}) collective-permute-start(bf16[8,4608]{1,0:T(8,128)(2,1)S(1)} %get-tuple-element.23), channel_id=1, source_target_pairs={{0,8},{1,9},{2,10},{3,11},{4,12},{5,13},{6,14},{7,15},{8,0},{9,1},... | collective-permute-start | bytes 221192 | tf_op jit(solution)/shard_map/ppermute | solution.py:239
  7.3 29.8 %copy-start.3 = (bf16[8,6144]{1,0:T(8,128)(2,1)S(1)}, bf16[8,6144]{1,0:T(8,128)(2,1)}, u32[]{:S(2)}) copy-start(bf16[8,6144]{1,0:T(8,128)(2,1)} %tok_ref.3) | copy-start | bytes 294916
  7.3 6.8 %collective-permute-start.6 = (bf16[8,4608]{1,0:T(8,128)(2,1)S(1)}, bf16[8,4608]{1,0:T(8,128)(2,1)S(1)}, u32[]{:S(2)}, u32[]{:S(2)}) collective-permute-start(bf16[8,4608]{1,0:T(8,128)(2,1)S(1)} %get-tuple-element.26.refs_6_), channel_id=1, source_target_pairs={{0,2},{1,3},{2,0},{3,1},{4,6},{5,7},{6,4},{7,5},{8,10},{9,11},{10,... | collective-permute-start | bytes 221192 | tf_op jit(solution)/shard_map/ppermute | solution.py:239
  8.9 5.1 %collective-permute-start.13 = (bf16[8,4608]{1,0:T(8,128)(2,1)S(1)}, bf16[8,4608]{1,0:T(8,128)(2,1)S(1)}, u32[]{:S(2)}, u32[]{:S(2)}) collective-permute-start(bf16[8,4608]{1,0:T(8,128)(2,1)S(1)} %get-tuple-element.26.refs_6_), channel_id=1, source_target_pairs={{0,1},{1,0},{2,3},{3,2},{4,5},{5,4},{6,7},{7,6},{8,9},{9,8},{10,11... | collective-permute-start | bytes 221192 | tf_op jit(solution)/shard_map/ppermute | solution.py:239
  9.8 4.8 %collective-permute-start.3 = (bf16[8,4608]{1,0:T(8,128)(2,1)S(1)}, bf16[8,4608]{1,0:T(8,128)(2,1)S(1)}, u32[]{:S(2)}, u32[]{:S(2)}) collective-permute-start(bf16[8,4608]{1,0:T(8,128)(2,1)S(1)} %collective-permute-done.2.refs_2_), channel_id=1, source_target_pairs={{0,2},{1,3},{2,0},{3,1},{4,6},{5,7},{6,4},{7,5},{8,10},{9,11},{10,... | collective-permute-start | bytes 221192 | tf_op jit(solution)/shard_map/ppermute | solution.py:239
  11.7 5.1 %collective-permute-start.5 = (bf16[8,4608]{1,0:T(8,128)(2,1)S(1)}, bf16[8,4608]{1,0:T(8,128)(2,1)S(1)}, u32[]{:S(2)}, u32[]{:S(2)}) collective-permute-start(bf16[8,4608]{1,0:T(8,128)(2,1)S(1)} %collective-permute-done.4.refs_4_), channel_id=1, source_target_pairs={{0,2},{1,3},{2,0},{3,1},{4,6},{5,7},{6,4},{7,5},{8,10},{9,11},{10,... | collective-permute-start | bytes 221192 | tf_op jit(solution)/shard_map/ppermute | solution.py:239
  13.3 4.4 %collective-permute-start.1 = (bf16[8,4608]{1,0:T(8,128)(2,1)S(1)}, bf16[8,4608]{1,0:T(8,128)(2,1)S(1)}, u32[]{:S(2)}, u32[]{:S(2)}) collective-permute-start(bf16[8,4608]{1,0:T(8,128)(2,1)S(1)} %collective-permute-done.refs_0_), channel_id=1, source_target_pairs={{0,2},{1,3},{2,0},{3,1},{4,6},{5,7},{6,4},{7,5},{8,10},{9,11},{10,... | collective-permute-start | bytes 221192 | tf_op jit(solution)/shard_map/ppermute | solution.py:239
  14.1 3.6 %collective-permute-start.14 = (bf16[8,4608]{1,0:T(8,128)(2,1)S(1)}, bf16[8,4608]{1,0:T(8,128)(2,1)S(1)}, u32[]{:S(2)}, u32[]{:S(2)}) collective-permute-start(bf16[8,4608]{1,0:T(8,128)(2,1)S(1)} %collective-permute-done.6.refs_7_), channel_id=1, source_target_pairs={{0,1},{1,0},{2,3},{3,2},{4,5},{5,4},{6,7},{7,6},{8,9},{9,8},{10,11... | collective-permute-start | bytes 221192 | tf_op jit(solution)/shard_map/ppermute | solution.py:239
  14.1 4.1 %collective-permute-start.11 = (bf16[8,4608]{1,0:T(8,128)(2,1)S(1)}, bf16[8,4608]{1,0:T(8,128)(2,1)S(1)}, u32[]{:S(2)}, u32[]{:S(2)}) collective-permute-start(bf16[8,4608]{1,0:T(8,128)(2,1)S(1)} %collective-permute-done.4.refs_4_), channel_id=1, source_target_pairs={{0,1},{1,0},{2,3},{3,2},{4,5},{5,4},{6,7},{7,6},{8,9},{9,8},{10,11... | collective-permute-start | bytes 221192 | tf_op jit(solution)/shard_map/ppermute | solution.py:239
  14.6 3.7 %collective-permute-start.7 = (bf16[8,4608]{1,0:T(8,128)(2,1)S(1)}, bf16[8,4608]{1,0:T(8,128)(2,1)S(1)}, u32[]{:S(2)}, u32[]{:S(2)}) collective-permute-start(bf16[8,4608]{1,0:T(8,128)(2,1)S(1)} %collective-permute-done.refs_0_), channel_id=1, source_target_pairs={{0,1},{1,0},{2,3},{3,2},{4,5},{5,4},{6,7},{7,6},{8,9},{9,8},{10,11... | collective-permute-start | bytes 221192 | tf_op jit(solution)/shard_map/ppermute | solution.py:239
  16.8 1.5 %collective-permute-start.9 = (bf16[8,4608]{1,0:T(8,128)(2,1)S(1)}, bf16[8,4608]{1,0:T(8,128)(2,1)S(1)}, u32[]{:S(2)}, u32[]{:S(2)}) collective-permute-start(bf16[8,4608]{1,0:T(8,128)(2,1)S(1)} %collective-permute-done.2.refs_2_), channel_id=1, source_target_pairs={{0,1},{1,0},{2,3},{3,2},{4,5},{5,4},{6,7},{7,6},{8,9},{9,8},{10,11... | collective-permute-start | bytes 221192 | tf_op jit(solution)/shard_map/ppermute | solution.py:239
  17.7 1.3 %collective-permute-start.10 = (bf16[8,4608]{1,0:T(8,128)(2,1)S(1)}, bf16[8,4608]{1,0:T(8,128)(2,1)S(1)}, u32[]{:S(2)}, u32[]{:S(2)}) collective-permute-start(bf16[8,4608]{1,0:T(8,128)(2,1)S(1)} %collective-permute-done.3.refs_3_), channel_id=1, source_target_pairs={{0,1},{1,0},{2,3},{3,2},{4,5},{5,4},{6,7},{7,6},{8,9},{9,8},{10,11... | collective-permute-start | bytes 221192 | tf_op jit(solution)/shard_map/ppermute | solution.py:239
  17.7 1.4 %collective-permute-start.12 = (bf16[8,4608]{1,0:T(8,128)(2,1)S(1)}, bf16[8,4608]{1,0:T(8,128)(2,1)S(1)}, u32[]{:S(2)}, u32[]{:S(2)}) collective-permute-start(bf16[8,4608]{1,0:T(8,128)(2,1)S(1)} %collective-permute-done.5.refs_5_), channel_id=1, source_target_pairs={{0,1},{1,0},{2,3},{3,2},{4,5},{5,4},{6,7},{7,6},{8,9},{9,8},{10,11... | collective-permute-start | bytes 221192 | tf_op jit(solution)/shard_map/ppermute | solution.py:239
  18.2 1.3 %collective-permute-start.8 = (bf16[8,4608]{1,0:T(8,128)(2,1)S(1)}, bf16[8,4608]{1,0:T(8,128)(2,1)S(1)}, u32[]{:S(2)}, u32[]{:S(2)}) collective-permute-start(bf16[8,4608]{1,0:T(8,128)(2,1)S(1)} %collective-permute-done.1.refs_1_), channel_id=1, source_target_pairs={{0,1},{1,0},{2,3},{3,2},{4,5},{5,4},{6,7},{7,6},{8,9},{9,8},{10,11... | collective-permute-start | bytes 221192 | tf_op jit(solution)/shard_map/ppermute | solution.py:239
  21.2 1.6 %collective-permute-start.19 = (bf16[32,4608]{1,0:T(8,128)(2,1)S(1)}, bf16[32,4608]{1,0:T(8,128)(2,1)S(1)}, u32[]{:S(2)}, u32[]{:S(2)}) collective-permute-start(bf16[32,4608]{1,0:T(8,128)(2,1)S(1)} %get-tuple-element.34), channel_id=1, source_target_pairs={{0,1},{1,0},{2,3},{3,2},{4,5},{5,4},{6,7},{7,6},{8,9},{9,8},{10,11... | collective-permute-start | bytes 884744 | tf_op jit(solution)/shard_map/ppermute | solution.py:239
  21.4 3.6 %collective-permute-start.15 = (bf16[32,4608]{1,0:T(8,128)(2,1)S(1)}, bf16[32,4608]{1,0:T(8,128)(2,1)S(1)}, u32[]{:S(2)}, u32[]{:S(2)}) collective-permute-start(bf16[32,4608]{1,0:T(8,128)(2,1)S(1)} %get-tuple-element.28), channel_id=1, source_target_pairs={{0,1},{1,0},{2,3},{3,2},{4,5},{5,4},{6,7},{7,6},{8,9},{9,8},{10,11... | collective-permute-start | bytes 884744 | tf_op jit(solution)/shard_map/ppermute | solution.py:239
  22.9 5.2 %collective-permute-start.22 = (bf16[8,4608]{1,0:T(8,128)(2,1)S(1)}, bf16[8,4608]{1,0:T(8,128)(2,1)S(1)}, u32[]{:S(2)}, u32[]{:S(2)}) collective-permute-start(bf16[8,4608]{1,0:T(8,128)(2,1)S(1)} %get-tuple-element.38), channel_id=1, source_target_pairs={{0,2},{1,3},{2,0},{3,1},{4,6},{5,7},{6,4},{7,5},{8,10},{9,11},{10,... | collective-permute-start | bytes 221192 | tf_op jit(solution)/shard_map/ppermute | solution.py:239
  24.1 6.7 %collective-permute-start.20 = (bf16[8,4608]{1,0:T(8,128)(2,1)S(1)}, bf16[8,4608]{1,0:T(8,128)(2,1)S(1)}, u32[]{:S(2)}, u32[]{:S(2)}) collective-permute-start(bf16[8,4608]{1,0:T(8,128)(2,1)S(1)} %get-tuple-element.36), channel_id=1, source_target_pairs={{0,2},{1,3},{2,0},{3,1},{4,6},{5,7},{6,4},{7,5},{8,10},{9,11},{10,... | collective-permute-start | bytes 221192 | tf_op jit(solution)/shard_map/ppermute | solution.py:239
  25.1 6.2 %collective-permute-start.17 = (bf16[8,4608]{1,0:T(8,128)(2,1)S(1)}, bf16[8,4608]{1,0:T(8,128)(2,1)S(1)}, u32[]{:S(2)}, u32[]{:S(2)}) collective-permute-start(bf16[8,4608]{1,0:T(8,128)(2,1)S(1)} %get-tuple-element.32), channel_id=1, source_target_pairs={{0,2},{1,3},{2,0},{3,1},{4,6},{5,7},{6,4},{7,5},{8,10},{9,11},{10,... | collective-permute-start | bytes 221192 | tf_op jit(solution)/shard_map/ppermute | solution.py:239
  26.3 7.4 %collective-permute-start.16 = (bf16[8,4608]{1,0:T(8,128)(2,1)S(1)}, bf16[8,4608]{1,0:T(8,128)(2,1)S(1)}, u32[]{:S(2)}, u32[]{:S(2)}) collective-permute-start(bf16[8,4608]{1,0:T(8,128)(2,1)S(1)} %get-tuple-element.30), channel_id=1, source_target_pairs={{0,2},{1,3},{2,0},{3,1},{4,6},{5,7},{6,4},{7,5},{8,10},{9,11},{10,... | collective-permute-start | bytes 221192 | tf_op jit(solution)/shard_map/ppermute | solution.py:239
  28.1 6.9 %collective-permute-start.23 = (bf16[8,4608]{1,0:T(8,128)(2,1)S(1)}, bf16[8,4608]{1,0:T(8,128)(2,1)S(1)}, u32[]{:S(2)}, u32[]{:S(2)}) collective-permute-start(bf16[8,4608]{1,0:T(8,128)(2,1)S(1)} %add.9), channel_id=1, source_target_pairs={{0,12},{1,13},{2,14},{3,15},{4,8},{5,9},{6,10},{7,11},{8,4},{9,5},... | collective-permute-start | bytes 221192 | tf_op jit(solution)/shard_map/ppermute | solution.py:239
  30.8 6.3 %collective-permute-start.21 = (bf16[8,4608]{1,0:T(8,128)(2,1)S(1)}, bf16[8,4608]{1,0:T(8,128)(2,1)S(1)}, u32[]{:S(2)}, u32[]{:S(2)}) collective-permute-start(bf16[8,4608]{1,0:T(8,128)(2,1)S(1)} %add.8), channel_id=1, source_target_pairs={{0,8},{1,9},{2,10},{3,11},{4,12},{5,13},{6,14},{7,15},{8,0},{9,1},... | collective-permute-start | bytes 221192 | tf_op jit(solution)/shard_map/ppermute | solution.py:239
  31.3 5.9 %collective-permute-start.18 = (bf16[8,4608]{1,0:T(8,128)(2,1)S(1)}, bf16[8,4608]{1,0:T(8,128)(2,1)S(1)}, u32[]{:S(2)}, u32[]{:S(2)}) collective-permute-start(bf16[8,4608]{1,0:T(8,128)(2,1)S(1)} %add.6), channel_id=1, source_target_pairs={{0,4},{1,5},{2,6},{3,7},{4,0},{5,1},{6,2},{7,3},{8,12},{9,13},{10,... | collective-permute-start | bytes 221192 | tf_op jit(solution)/shard_map/ppermute | solution.py:239

commit v3 on v2

--- a/solution.py
+++ b/solution.py
@@ -117,8 +117,8 @@
 
 def ffn_kernel(count, *refs):
     pieces = refs[:count]
-    wg_ref, wu_ref, wd_ref = refs[count : count + 3]
-    outs, x_ref = refs[count + 3 : -1], refs[-1]
+    weights = [refs[n : n + 3] for n in range(count, count + 3 * CORES, 3)]
+    outs, x_ref = refs[count + 3 * CORES : -1], refs[-1]
     total, width = x_ref.shape
     main, tail, blocks = packing(width)
     spare = SUB - CAP
@@ -136,11 +136,16 @@
     def chunk(base):
         rows = pl.ds(base, size)
         x = x_ref[rows, :]
-        gate = dot(x, wg_ref[...])
-        up = dot(x, wu_ref[...])
-        hidden = (gate / (1.0 + jnp.exp(-gate)) * up).astype(BF16)
+        hidden = []
+        for wg_ref, wu_ref, _ in weights:
+            gate = dot(x, wg_ref[...])
+            up = dot(x, wu_ref[...])
+            hidden.append((gate / (1.0 + jnp.exp(-gate)) * up).astype(BF16))
         for cut in cuts + [slice(main, width)]:
-            x_ref[rows, cut] = dot(hidden, wd_ref[:, cut]).astype(BF16)
+            result = dot(hidden[0], weights[0][2][:, cut])
+            for h, w in zip(hidden[1:], weights[1:]):
+                result = result + dot(h, w[2][:, cut])
+            x_ref[rows, cut] = result.astype(BF16)
 
     if total == size:
         chunk(0)
@@ -160,7 +165,7 @@
     return pl.pallas_call(
         functools.partial(ffn_kernel, len(pieces)),
         out_shape=[pltpu.VMEM((n, main), BF16) for n in sizes],
-        in_specs=[VMEM] * (len(pieces) + 3),
+        in_specs=[VMEM] * (len(pieces) + len(weights)),
         out_specs=[VMEM] * len(sizes),
         scratch_shapes=[pltpu.VMEM((total, width), BF16)],
         compiler_params=room(24),
@@ -239,28 +244,20 @@
         return lax.ppermute(value, "expert", [(i, i ^ distance) for i in range(devices)])
 
     *outgoing, table = pre(tokens, norm_gain, router, expert_ids, members)
-    weights = [w_gate, w_up, w_down]
+    weights = [w_gate, w_up, w_down] + [swap(w, 1) for w in (w_gate, w_up, w_down)]
 
     here = {}
     for k in range(experts):
-        here[0, k, 0] = swap(outgoing[k], k * members) if k else outgoing[0]
+        here[k, 0] = swap(outgoing[k], k * members) if k else outgoing[0]
     for k in range(experts):
         for y in range(1, lines):
-            here[0, k, y] = swap(here[0, k, 0], y * CORES)
+            here[k, y] = swap(here[k, 0], y * CORES)
+    order = [(k, y) for k in range(experts) for y in range(lines)]
+    results = dict(zip(order, ffn([here[o] for o in order], weights, [SUB] * len(order))))
+
+    half = {}
     for k in range(experts):
-        for y in range(lines):
-            here[1, k, y] = swap(here[0, k, y], 1)
-    groups = [list(range(experts // 2, experts)), list(range(experts // 2 - 1, -1, -1))]
-    order = [(c, k, y) for c in range(CORES) for g in groups for k in g for y in range(lines)]
-    results = ffn([here[o] for o in order], weights, [len(g) * lines * SUB for _ in range(CORES) for g in groups])
-
-    half = {}
-    for n, group in enumerate(groups):
-        keep, give = results[n], results[len(groups) + n]
-        parts = add([keep, swap(give, 1)], len(group) * lines)
-        for m, k in enumerate(group):
-            mine, theirs = parts[m * lines], parts[m * lines + 1 : (m + 1) * lines]
-            half[k] = [mine] + [swap(p, (y + 1) * CORES) for y, p in enumerate(theirs)]
+        half[k] = [results[k, 0]] + [swap(results[k, y], y * CORES) for y in range(1, lines)]
     home = list(half[0])
     for k in range(1, experts):
         (total,) = add(half[k], 1)

time: 38.2 us -> 43 us (1.13)
  starting transfers between devices: 21.9 us -> 27.3 us
  waiting for transfers between devices: 11.1 us -> 8.78 us
  Pallas kernels: 4.28 us -> 6 us
    ppermute x24 -> x17, starting transfers between devices: 21.9 us -> 27.3 us  [swap(): lax.ppermute(value, 'expert', [(i, i ^ distance) for i in range(devices)])]
    ppermute x24 -> x17, waiting for transfers between devices: 11.1 us -> 8.78 us  [swap(): lax.ppermute(value, 'expert', [(i, i ^ distance) for i in range(devices)])]
    pallas_call x1, Pallas kernels: 1.68 us -> 3.53 us  [ffn(): pl.pallas_call(functools.partial(ffn_kernel, len(pieces)), out_shape=[plt...]
  transfers between devices with their start and end apart: 24 -> 17, of which waited for: 12 -> 7; matrix products, arithmetic and copies ran while one was open for 0% -> 0% of each run, Pallas kernels for 1% -> 4%
where the time goes in v3:
time: 43 us; the launch traced here: 42.9 us
  starting transfers between devices  27.3 us (63%)
  waiting for transfers between devices  8.78 us (20%)
  Pallas kernels  6 us (14%)
  between operations  0.76 us (2%)
    ppermute x17, starting transfers between devices, swap(): lax.ppermute(value, 'expert', [(i, i ^ distance) for i in range(devices)])  27.3 us
    ppermute x17, waiting for transfers between devices, swap(): lax.ppermute(value, 'expert', [(i, i ^ distance) for i in range(devices)])  8.78 us
    pallas_call x1, Pallas kernels, ffn(): pl.pallas_call(functools.partial(ffn_kernel, len(pieces)), out_shape=[plt...  3.53 us
    pallas_call x1, Pallas kernels, pre(): pl.pallas_call(functools.partial(pre_kernel, experts, members), out_shape...  1.47 us
    pallas_call x1, Pallas kernels, combine(): pl.pallas_call(functools.partial(combine_kernel, experts), out_shape=jax....  0.93 us
  transfers between devices with their start and end apart: 17, of which 7 were waited for; matrix products, arithmetic and copies ran while one was open for 0% of the time, Pallas kernels for 4%

profile of v3, /device:TPU:0, one launch (start us, length us, event | category | flops | bytes accessed | tf_op | source)
XLA Modules:
  0.0 42.9 jit_solution(14815172838207132956)
XLA Ops:
  0.0 0.5 %collective-permute-start.7 = (bf16[6144,256]{1,0:T(8,128)(2,1)}, bf16[6144,256]{1,0:T(8,128)(2,1)S(1)}, u32[]{:S(2)}, u32[]{:S(2)}) collective-permute-start(bf16[6144,256]{1,0:T(8,128)(2,1)} %refs_8_.1), channel_id=1, source_target_pairs={{0,1},{1,0},{2,3},{3,2},{4,5},{5,4},{6,7},{7,6},{8,9},{9,8},{10,11... | collective-permute-start | bytes 9437192 | tf_op jit(solution)/shard_map/ppermute | solution.py:244
  0.5 0.0 collective-permute-start.8
  0.5 0.5 %collective-permute-start.9 = (bf16[256,6144]{1,0:T(8,128)(2,1)}, bf16[256,6144]{1,0:T(8,128)(2,1)S(1)}, u32[]{:S(2)}, u32[]{:S(2)}) collective-permute-start(bf16[256,6144]{1,0:T(8,128)(2,1)} %refs_10_.1), channel_id=1, source_target_pairs={{0,1},{1,0},{2,3},{3,2},{4,5},{5,4},{6,7},{7,6},{8,9},{9,8},{10,11... | collective-permute-start | bytes 9437192 | tf_op jit(solution)/shard_map/ppermute | solution.py:244
  1.0 0.0 copy-start
  1.0 0.0 copy-start.1
  1.0 0.0 copy-start.2
  1.0 1.5 %pre.1 = (bf16[8,4608]{1,0:T(8,128)(2,1)S(1)}, bf16[8,4608]{1,0:T(8,128)(2,1)S(1)}, bf16[8,4608]{1,0:T(8,128)(2,1)S(1)}, bf16[8,4608]{1,0:T(8,128)(2,1)S(1)}, f32[8,128]{1,0:T(8,128)S(1)}) custom-call(s32[2,8]{1,0:T(2,128)} %bitcast.5, bf16[8,6144]{1,0:T(8,128)(2,1)} %tok_ref.3, f32[1,6144]{1,0:T(1,128)} %bitcast.4, bf16[4,6144]{1,0:T(4,128)(2,1)} %bitcast.3), custom_call_target="tpu_custom_call" | custom-call | flops 20000000000 | bytes 40000000 | tf_op jit(solution)/shard_map/pre/pallas_call | solution.py:107
  2.5 2.6 %collective-permute-start.1 = (bf16[8,4608]{1,0:T(8,128)(2,1)S(1)}, bf16[8,4608]{1,0:T(8,128)(2,1)S(1)}, u32[]{:S(2)}, u32[]{:S(2)}) collective-permute-start(bf16[8,4608]{1,0:T(8,128)(2,1)S(1)} %get-tuple-element.20), channel_id=1, source_target_pairs={{0,4},{1,5},{2,6},{3,7},{4,0},{5,1},{6,2},{7,3},{8,12},{9,13},{10,... | collective-permute-start | bytes 221192 | tf_op jit(solution)/shard_map/ppermute | solution.py:244
  5.1 2.6 %collective-permute-start.3 = (bf16[8,4608]{1,0:T(8,128)(2,1)S(1)}, bf16[8,4608]{1,0:T(8,128)(2,1)S(1)}, u32[]{:S(2)}, u32[]{:S(2)}) collective-permute-start(bf16[8,4608]{1,0:T(8,128)(2,1)S(1)} %get-tuple-element.21), channel_id=1, source_target_pairs={{0,8},{1,9},{2,10},{3,11},{4,12},{5,13},{6,14},{7,15},{8,0},{9,1},... | collective-permute-start | bytes 221192 | tf_op jit(solution)/shard_map/ppermute | solution.py:244
  7.7 0.3 collective-permute-done.1.refs_2_
  8.1 4.8 %collective-permute-start.5 = (bf16[8,4608]{1,0:T(8,128)(2,1)S(1)}, bf16[8,4608]{1,0:T(8,128)(2,1)S(1)}, u32[]{:S(2)}, u32[]{:S(2)}) collective-permute-start(bf16[8,4608]{1,0:T(8,128)(2,1)S(1)} %get-tuple-element.22), channel_id=1, source_target_pairs={{0,12},{1,13},{2,14},{3,15},{4,8},{5,9},{6,10},{7,11},{8,4},{9,5},... | collective-permute-start | bytes 221192 | tf_op jit(solution)/shard_map/ppermute | solution.py:244
  12.9 0.0 collective-permute-done.3.refs_4_
  12.9 0.0 copy-start.3
  12.9 1.5 %collective-permute-start = (bf16[8,4608]{1,0:T(8,128)(2,1)S(1)}, bf16[8,4608]{1,0:T(8,128)(2,1)S(1)}, u32[]{:S(2)}, u32[]{:S(2)}) collective-permute-start(bf16[8,4608]{1,0:T(8,128)(2,1)S(1)} %get-tuple-element.19.refs_0_), channel_id=1, source_target_pairs={{0,2},{1,3},{2,0},{3,1},{4,6},{5,7},{6,4},{7,5},{8,10},{9,11},{10,... | collective-permute-start | bytes 221192 | tf_op jit(solution)/shard_map/ppermute | solution.py:244
  14.4 0.8 %collective-permute-done.5.refs_6_ = bf16[8,4608]{1,0:T(8,128)(2,1)S(1)} collective-permute-done((bf16[8,4608]{1,0:T(8,128)(2,1)S(1)}, bf16[8,4608]{1,0:T(8,128)(2,1)S(1)}, u32[]{:S(2)}, u32[]{:S(2)}) %collective-permute-start.5) | collective-permute-done | bytes 73760 | tf_op jit(solution)/shard_map/ppermute | solution.py:244
  15.2 1.5 %collective-permute-start.2 = (bf16[8,4608]{1,0:T(8,128)(2,1)S(1)}, bf16[8,4608]{1,0:T(8,128)(2,1)S(1)}, u32[]{:S(2)}, u32[]{:S(2)}) collective-permute-start(bf16[8,4608]{1,0:T(8,128)(2,1)S(1)} %collective-permute-done.1.refs_2_), channel_id=1, source_target_pairs={{0,2},{1,3},{2,0},{3,1},{4,6},{5,7},{6,4},{7,5},{8,10},{9,11},{10,... | collective-permute-start | bytes 221192 | tf_op jit(solution)/shard_map/ppermute | solution.py:244
  16.7 0.5 %collective-permute-done.refs_1_ = bf16[8,4608]{1,0:T(8,128)(2,1)S(1)} collective-permute-done((bf16[8,4608]{1,0:T(8,128)(2,1)S(1)}, bf16[8,4608]{1,0:T(8,128)(2,1)S(1)}, u32[]{:S(2)}, u32[]{:S(2)}) %collective-permute-start) | collective-permute-done | bytes 73760 | tf_op jit(solution)/shard_map/ppermute | solution.py:244
  17.3 1.5 %collective-permute-start.4 = (bf16[8,4608]{1,0:T(8,128)(2,1)S(1)}, bf16[8,4608]{1,0:T(8,128)(2,1)S(1)}, u32[]{:S(2)}, u32[]{:S(2)}) collective-permute-start(bf16[8,4608]{1,0:T(8,128)(2,1)S(1)} %collective-permute-done.3.refs_4_), channel_id=1, source_target_pairs={{0,2},{1,3},{2,0},{3,1},{4,6},{5,7},{6,4},{7,5},{8,10},{9,11},{10,... | collective-permute-start | bytes 221192 | tf_op jit(solution)/shard_map/ppermute | solution.py:244
  18.8 1.5 %collective-permute-done.2.refs_3_ = bf16[8,4608]{1,0:T(8,128)(2,1)S(1)} collective-permute-done((bf16[8,4608]{1,0:T(8,128)(2,1)S(1)}, bf16[8,4608]{1,0:T(8,128)(2,1)S(1)}, u32[]{:S(2)}, u32[]{:S(2)}) %collective-permute-start.2) | collective-permute-done | bytes 73760 | tf_op jit(solution)/shard_map/ppermute | solution.py:244
  20.3 1.6 %collective-permute-start.6 = (bf16[8,4608]{1,0:T(8,128)(2,1)S(1)}, bf16[8,4608]{1,0:T(8,128)(2,1)S(1)}, u32[]{:S(2)}, u32[]{:S(2)}) collective-permute-start(bf16[8,4608]{1,0:T(8,128)(2,1)S(1)} %collective-permute-done.5.refs_6_), channel_id=1, source_target_pairs={{0,2},{1,3},{2,0},{3,1},{4,6},{5,7},{6,4},{7,5},{8,10},{9,11},{10,... | collective-permute-start | bytes 221192 | tf_op jit(solution)/shard_map/ppermute | solution.py:244
  21.8 0.0 collective-permute-done.4.refs_5_
  21.8 2.8 %collective-permute-done.6.refs_7_ = bf16[8,4608]{1,0:T(8,128)(2,1)S(1)} collective-permute-done((bf16[8,4608]{1,0:T(8,128)(2,1)S(1)}, bf16[8,4608]{1,0:T(8,128)(2,1)S(1)}, u32[]{:S(2)}, u32[]{:S(2)}) %collective-permute-start.6) | collective-permute-done | bytes 73760 | tf_op jit(solution)/shard_map/ppermute | solution.py:244
  24.6 0.0 collective-permute-done.7.refs_11_
  24.6 0.0 collective-permute-done.8.refs_12_
  24.6 0.0 collective-permute-done.9.refs_13_
  24.6 0.0 copy-done
  24.6 0.0 copy-done.1
  24.7 0.0 copy-done.2
  24.7 3.5 %ffn.1 = (bf16[8,4608]{1,0:T(8,128)(2,1)S(1)}, bf16[8,4608]{1,0:T(8,128)(2,1)S(1)}, bf16[8,4608]{1,0:T(8,128)(2,1)S(1)}, bf16[8,4608]{1,0:T(8,128)(2,1)S(1)}, bf...) custom-call(bf16[8,4608]{1,0:T(8,128)(2,1)S(1)} %get-tuple-element.1, ...), custom_call_target="tpu_custom_call" | custom-call | tf_op jit(solution)/shard_map/ffn/pallas_call | solution.py:165
  28.2 1.6 %collective-permute-start.15 = (bf16[8,4608]{1,0:T(8,128)(2,1)S(1)}, bf16[8,4608]{1,0:T(8,128)(2,1)S(1)}, u32[]{:S(2)}, u32[]{:S(2)}) collective-permute-start(bf16[8,4608]{1,0:T(8,128)(2,1)S(1)} %get-tuple-element.30), channel_id=1, source_target_pairs={{0,2},{1,3},{2,0},{3,1},{4,6},{5,7},{6,4},{7,5},{8,10},{9,11},{10,... | collective-permute-start | bytes 221192 | tf_op jit(solution)/shard_map/ppermute | solution.py:244
  29.8 0.5 %collective-permute-start.13 = (bf16[8,4608]{1,0:T(8,128)(2,1)S(1)}, bf16[8,4608]{1,0:T(8,128)(2,1)S(1)}, u32[]{:S(2)}, u32[]{:S(2)}) collective-permute-start(bf16[8,4608]{1,0:T(8,128)(2,1)S(1)} %get-tuple-element.28), channel_id=1, source_target_pairs={{0,2},{1,3},{2,0},{3,1},{4,6},{5,7},{6,4},{7,5},{8,10},{9,11},{10,... | collective-permute-start | bytes 221192 | tf_op jit(solution)/shard_map/ppermute | solution.py:244
  30.3 1.6 %collective-permute-start.11 = (bf16[8,4608]{1,0:T(8,128)(2,1)S(1)}, bf16[8,4608]{1,0:T(8,128)(2,1)S(1)}, u32[]{:S(2)}, u32[]{:S(2)}) collective-permute-start(bf16[8,4608]{1,0:T(8,128)(2,1)S(1)} %get-tuple-element.26), channel_id=1, source_target_pairs={{0,2},{1,3},{2,0},{3,1},{4,6},{5,7},{6,4},{7,5},{8,10},{9,11},{10,... | collective-permute-start | bytes 221192 | tf_op jit(solution)/shard_map/ppermute | solution.py:244
  31.9 0.5 %collective-permute-start.10 = (bf16[8,4608]{1,0:T(8,128)(2,1)S(1)}, bf16[8,4608]{1,0:T(8,128)(2,1)S(1)}, u32[]{:S(2)}, u32[]{:S(2)}) collective-permute-start(bf16[8,4608]{1,0:T(8,128)(2,1)S(1)} %get-tuple-element.24), channel_id=1, source_target_pairs={{0,2},{1,3},{2,0},{3,1},{4,6},{5,7},{6,4},{7,5},{8,10},{9,11},{10,... | collective-permute-start | bytes 221192 | tf_op jit(solution)/shard_map/ppermute | solution.py:244
  32.3 0.3 collective-permute-done.15.refs_1_
  32.7 4.0 %collective-permute-start.16 = (bf16[8,4608]{1,0:T(8,128)(2,1)S(1)}, bf16[8,4608]{1,0:T(8,128)(2,1)S(1)}, u32[]{:S(2)}, u32[]{:S(2)}) collective-permute-start(bf16[8,4608]{1,0:T(8,128)(2,1)S(1)} %add.5), channel_id=1, source_target_pairs={{0,12},{1,13},{2,14},{3,15},{4,8},{5,9},{6,10},{7,11},{8,4},{9,5},... | collective-permute-start | bytes 221192 | tf_op jit(solution)/shard_map/ppermute | solution.py:244
  36.6 0.0 collective-permute-done.13.refs_1_
  36.6 0.1 collective-permute-start.14
  36.7 0.0 collective-permute-done.11.refs_1_
  36.8 2.0 %collective-permute-start.12 = (bf16[8,4608]{1,0:T(8,128)(2,1)S(1)}, bf16[8,4608]{1,0:T(8,128)(2,1)S(1)}, u32[]{:S(2)}, u32[]{:S(2)}) collective-permute-start(bf16[8,4608]{1,0:T(8,128)(2,1)S(1)} %add.3), channel_id=1, source_target_pairs={{0,4},{1,5},{2,6},{3,7},{4,0},{5,1},{6,2},{7,3},{8,12},{9,13},{10,... | collective-permute-start | bytes 221192 | tf_op jit(solution)/shard_map/ppermute | solution.py:244
  39.4 0.0 collective-permute-done.10.refs_1_
  39.4 0.0 collective-permute-done.16.refs_4_
  39.5 2.5 %collective-permute-done.14.refs_3_ = bf16[8,4608]{1,0:T(8,128)(2,1)S(1)} collective-permute-done((bf16[8,4608]{1,0:T(8,128)(2,1)S(1)}, bf16[8,4608]{1,0:T(8,128)(2,1)S(1)}, u32[]{:S(2)}, u32[]{:S(2)}) %collective-permute-start.14) | collective-permute-done | bytes 73760 | tf_op jit(solution)/shard_map/ppermute | solution.py:244
  42.0 0.0 collective-permute-done.12.refs_2_
  42.0 0.0 copy-done.3
  42.0 0.9 %combine.1 = bf16[8,6144]{1,0:T(8,128)(2,1)} custom-call(s32[1]{0:T(128)S(6)} %copy.9.live_ref, f32[8,128]{1,0:T(8,128)S(1)} %get-tuple-element.18.table_ref, bf16[8,6144]{1,0:T(8,128)(2,1)S(1)} %copy-done.3, bf16[8,4608]{1,0:T(8,128)(2,1)S(1)} %get-tuple-element.23.refs_0_, bf16[8,4608]{1,0:T(8,128)(2,1)S(1)} %collective-permute-done.10.refs_1_, ...), custom_call_target="tpu_custom_call" | custom-call | tf_op jit(solution)/shard_map/combine/pallas_call | solution.py:227
  (3 shorter events, 0.1 us)
Async XLA Ops:
  0.0 24.6 %collective-permute-start.7 = (bf16[6144,256]{1,0:T(8,128)(2,1)}, bf16[6144,256]{1,0:T(8,128)(2,1)S(1)}, u32[]{:S(2)}, u32[]{:S(2)}) collective-permute-start(bf16[6144,256]{1,0:T(8,128)(2,1)} %refs_8_.1), channel_id=1, source_target_pairs={{0,1},{1,0},{2,3},{3,2},{4,5},{5,4},{6,7},{7,6},{8,9},{9,8},{10,11... | collective-permute-start | bytes 9437192 | tf_op jit(solution)/shard_map/ppermute | solution.py:244
  0.5 24.1 %collective-permute-start.8 = (bf16[6144,256]{1,0:T(8,128)(2,1)}, bf16[6144,256]{1,0:T(8,128)(2,1)S(1)}, u32[]{:S(2)}, u32[]{:S(2)}) collective-permute-start(bf16[6144,256]{1,0:T(8,128)(2,1)} %refs_9_.1), channel_id=1, source_target_pairs={{0,1},{1,0},{2,3},{3,2},{4,5},{5,4},{6,7},{7,6},{8,9},{9,8},{10,11... | collective-permute-start | bytes 9437192 | tf_op jit(solution)/shard_map/ppermute | solution.py:244
  0.5 24.1 %collective-permute-start.9 = (bf16[256,6144]{1,0:T(8,128)(2,1)}, bf16[256,6144]{1,0:T(8,128)(2,1)S(1)}, u32[]{:S(2)}, u32[]{:S(2)}) collective-permute-start(bf16[256,6144]{1,0:T(8,128)(2,1)} %refs_10_.1), channel_id=1, source_target_pairs={{0,1},{1,0},{2,3},{3,2},{4,5},{5,4},{6,7},{7,6},{8,9},{9,8},{10,11... | collective-permute-start | bytes 9437192 | tf_op jit(solution)/shard_map/ppermute | solution.py:244
  1.0 23.6 %copy-start = (bf16[6144,256]{1,0:T(8,128)(2,1)S(1)}, bf16[6144,256]{1,0:T(8,128)(2,1)}, u32[]{:S(2)}) copy-start(bf16[6144,256]{1,0:T(8,128)(2,1)} %refs_8_.1) | copy-start | bytes 9437188
  1.0 23.6 %copy-start.1 = (bf16[6144,256]{1,0:T(8,128)(2,1)S(1)}, bf16[6144,256]{1,0:T(8,128)(2,1)}, u32[]{:S(2)}) copy-start(bf16[6144,256]{1,0:T(8,128)(2,1)} %refs_9_.1) | copy-start | bytes 9437188
  1.0 23.7 %copy-start.2 = (bf16[256,6144]{1,0:T(8,128)(2,1)S(1)}, bf16[256,6144]{1,0:T(8,128)(2,1)}, u32[]{:S(2)}) copy-start(bf16[256,6144]{1,0:T(8,128)(2,1)} %refs_10_.1) | copy-start | bytes 9437188
  2.5 5.6 %collective-permute-start.1 = (bf16[8,4608]{1,0:T(8,128)(2,1)S(1)}, bf16[8,4608]{1,0:T(8,128)(2,1)S(1)}, u32[]{:S(2)}, u32[]{:S(2)}) collective-permute-start(bf16[8,4608]{1,0:T(8,128)(2,1)S(1)} %get-tuple-element.20), channel_id=1, source_target_pairs={{0,4},{1,5},{2,6},{3,7},{4,0},{5,1},{6,2},{7,3},{8,12},{9,13},{10,... | collective-permute-start | bytes 221192 | tf_op jit(solution)/shard_map/ppermute | solution.py:244
  5.1 7.8 %collective-permute-start.3 = (bf16[8,4608]{1,0:T(8,128)(2,1)S(1)}, bf16[8,4608]{1,0:T(8,128)(2,1)S(1)}, u32[]{:S(2)}, u32[]{:S(2)}) collective-permute-start(bf16[8,4608]{1,0:T(8,128)(2,1)S(1)} %get-tuple-element.21), channel_id=1, source_target_pairs={{0,8},{1,9},{2,10},{3,11},{4,12},{5,13},{6,14},{7,15},{8,0},{9,1},... | collective-permute-start | bytes 221192 | tf_op jit(solution)/shard_map/ppermute | solution.py:244
  8.1 7.2 %collective-permute-start.5 = (bf16[8,4608]{1,0:T(8,128)(2,1)S(1)}, bf16[8,4608]{1,0:T(8,128)(2,1)S(1)}, u32[]{:S(2)}, u32[]{:S(2)}) collective-permute-start(bf16[8,4608]{1,0:T(8,128)(2,1)S(1)} %get-tuple-element.22), channel_id=1, source_target_pairs={{0,12},{1,13},{2,14},{3,15},{4,8},{5,9},{6,10},{7,11},{8,4},{9,5},... | collective-permute-start | bytes 221192 | tf_op jit(solution)/shard_map/ppermute | solution.py:244
  12.9 29.1 %copy-start.3 = (bf16[8,6144]{1,0:T(8,128)(2,1)S(1)}, bf16[8,6144]{1,0:T(8,128)(2,1)}, u32[]{:S(2)}) copy-start(bf16[8,6144]{1,0:T(8,128)(2,1)} %tok_ref.3) | copy-start | bytes 294916
  12.9 4.4 %collective-permute-start = (bf16[8,4608]{1,0:T(8,128)(2,1)S(1)}, bf16[8,4608]{1,0:T(8,128)(2,1)S(1)}, u32[]{:S(2)}, u32[]{:S(2)}) collective-permute-start(bf16[8,4608]{1,0:T(8,128)(2,1)S(1)} %get-tuple-element.19.refs_0_), channel_id=1, source_target_pairs={{0,2},{1,3},{2,0},{3,1},{4,6},{5,7},{6,4},{7,5},{8,10},{9,11},{10,... | collective-permute-start | bytes 221192 | tf_op jit(solution)/shard_map/ppermute | solution.py:244
  15.2 5.0 %collective-permute-start.2 = (bf16[8,4608]{1,0:T(8,128)(2,1)S(1)}, bf16[8,4608]{1,0:T(8,128)(2,1)S(1)}, u32[]{:S(2)}, u32[]{:S(2)}) collective-permute-start(bf16[8,4608]{1,0:T(8,128)(2,1)S(1)} %collective-permute-done.1.refs_2_), channel_id=1, source_target_pairs={{0,2},{1,3},{2,0},{3,1},{4,6},{5,7},{6,4},{7,5},{8,10},{9,11},{10,... | collective-permute-start | bytes 221192 | tf_op jit(solution)/shard_map/ppermute | solution.py:244
  17.3 4.6 %collective-permute-start.4 = (bf16[8,4608]{1,0:T(8,128)(2,1)S(1)}, bf16[8,4608]{1,0:T(8,128)(2,1)S(1)}, u32[]{:S(2)}, u32[]{:S(2)}) collective-permute-start(bf16[8,4608]{1,0:T(8,128)(2,1)S(1)} %collective-permute-done.3.refs_4_), channel_id=1, source_target_pairs={{0,2},{1,3},{2,0},{3,1},{4,6},{5,7},{6,4},{7,5},{8,10},{9,11},{10,... | collective-permute-start | bytes 221192 | tf_op jit(solution)/shard_map/ppermute | solution.py:244
  20.3 4.4 %collective-permute-start.6 = (bf16[8,4608]{1,0:T(8,128)(2,1)S(1)}, bf16[8,4608]{1,0:T(8,128)(2,1)S(1)}, u32[]{:S(2)}, u32[]{:S(2)}) collective-permute-start(bf16[8,4608]{1,0:T(8,128)(2,1)S(1)} %collective-permute-done.5.refs_6_), channel_id=1, source_target_pairs={{0,2},{1,3},{2,0},{3,1},{4,6},{5,7},{6,4},{7,5},{8,10},{9,11},{10,... | collective-permute-start | bytes 221192 | tf_op jit(solution)/shard_map/ppermute | solution.py:244
  28.2 4.4 %collective-permute-start.15 = (bf16[8,4608]{1,0:T(8,128)(2,1)S(1)}, bf16[8,4608]{1,0:T(8,128)(2,1)S(1)}, u32[]{:S(2)}, u32[]{:S(2)}) collective-permute-start(bf16[8,4608]{1,0:T(8,128)(2,1)S(1)} %get-tuple-element.30), channel_id=1, source_target_pairs={{0,2},{1,3},{2,0},{3,1},{4,6},{5,7},{6,4},{7,5},{8,10},{9,11},{10,... | collective-permute-start | bytes 221192 | tf_op jit(solution)/shard_map/ppermute | solution.py:244
  29.8 6.8 %collective-permute-start.13 = (bf16[8,4608]{1,0:T(8,128)(2,1)S(1)}, bf16[8,4608]{1,0:T(8,128)(2,1)S(1)}, u32[]{:S(2)}, u32[]{:S(2)}) collective-permute-start(bf16[8,4608]{1,0:T(8,128)(2,1)S(1)} %get-tuple-element.28), channel_id=1, source_target_pairs={{0,2},{1,3},{2,0},{3,1},{4,6},{5,7},{6,4},{7,5},{8,10},{9,11},{10,... | collective-permute-start | bytes 221192 | tf_op jit(solution)/shard_map/ppermute | solution.py:244
  30.3 6.4 %collective-permute-start.11 = (bf16[8,4608]{1,0:T(8,128)(2,1)S(1)}, bf16[8,4608]{1,0:T(8,128)(2,1)S(1)}, u32[]{:S(2)}, u32[]{:S(2)}) collective-permute-start(bf16[8,4608]{1,0:T(8,128)(2,1)S(1)} %get-tuple-element.26), channel_id=1, source_target_pairs={{0,2},{1,3},{2,0},{3,1},{4,6},{5,7},{6,4},{7,5},{8,10},{9,11},{10,... | collective-permute-start | bytes 221192 | tf_op jit(solution)/shard_map/ppermute | solution.py:244
  31.9 7.6 %collective-permute-start.10 = (bf16[8,4608]{1,0:T(8,128)(2,1)S(1)}, bf16[8,4608]{1,0:T(8,128)(2,1)S(1)}, u32[]{:S(2)}, u32[]{:S(2)}) collective-permute-start(bf16[8,4608]{1,0:T(8,128)(2,1)S(1)} %get-tuple-element.24), channel_id=1, source_target_pairs={{0,2},{1,3},{2,0},{3,1},{4,6},{5,7},{6,4},{7,5},{8,10},{9,11},{10,... | collective-permute-start | bytes 221192 | tf_op jit(solution)/shard_map/ppermute | solution.py:244
  32.7 6.8 %collective-permute-start.16 = (bf16[8,4608]{1,0:T(8,128)(2,1)S(1)}, bf16[8,4608]{1,0:T(8,128)(2,1)S(1)}, u32[]{:S(2)}, u32[]{:S(2)}) collective-permute-start(bf16[8,4608]{1,0:T(8,128)(2,1)S(1)} %add.5), channel_id=1, source_target_pairs={{0,12},{1,13},{2,14},{3,15},{4,8},{5,9},{6,10},{7,11},{8,4},{9,5},... | collective-permute-start | bytes 221192 | tf_op jit(solution)/shard_map/ppermute | solution.py:244
  36.6 5.3 %collective-permute-start.14 = (bf16[8,4608]{1,0:T(8,128)(2,1)S(1)}, bf16[8,4608]{1,0:T(8,128)(2,1)S(1)}, u32[]{:S(2)}, u32[]{:S(2)}) collective-permute-start(bf16[8,4608]{1,0:T(8,128)(2,1)S(1)} %add.4), channel_id=1, source_target_pairs={{0,8},{1,9},{2,10},{3,11},{4,12},{5,13},{6,14},{7,15},{8,0},{9,1},... | collective-permute-start | bytes 221192 | tf_op jit(solution)/shard_map/ppermute | solution.py:244
  36.8 5.2 %collective-permute-start.12 = (bf16[8,4608]{1,0:T(8,128)(2,1)S(1)}, bf16[8,4608]{1,0:T(8,128)(2,1)S(1)}, u32[]{:S(2)}, u32[]{:S(2)}) collective-permute-start(bf16[8,4608]{1,0:T(8,128)(2,1)S(1)} %add.3), channel_id=1, source_target_pairs={{0,4},{1,5},{2,6},{3,7},{4,0},{5,1},{6,2},{7,3},{8,12},{9,13},{10,... | collective-permute-start | bytes 221192 | tf_op jit(solution)/shard_map/ppermute | solution.py:244
